TPU v7x, 8 devices: a whole 2x2x1 slice. The times are simulated.
8 devices in a mesh: dp: 1 (over z), sp: 8 (over y, x, core).
Axes of the slice: x: 2, y: 2, z: 1, core: 2. Of those that a mesh axis runs over, the one named last changes fastest.
Arguments:
- hidden: bfloat16 [6144, 3072], P(('dp', 'sp'))
- positions: int32 [6144], P(('dp', 'sp'))
- d_attn: bfloat16 [6144, 3072], P(('dp', 'sp'))
- ln_weight: bfloat16 [3072], replicated
- w_q: bfloat16 [3072, 3072], replicated
- w_k: bfloat16 [3072, 1024], replicated
- w_v: bfloat16 [3072, 1024], replicated
- w_o: bfloat16 [3072, 3072], replicated
Outputs:
- output 1: bfloat16 [6144, 3072], P(('dp', 'sp'))
- output 2: bfloat16 [6144, 3072], P(('dp', 'sp'))
- output 3: bfloat16 [3072], P('dp')
- output 4: bfloat16 [3072, 3072], P('dp')
- output 5: bfloat16 [3072, 1024], P('dp')
- output 6: bfloat16 [3072, 1024], P('dp')
- output 7: bfloat16 [3072, 3072], P('dp')
All inputs are finite; a program needn't handle non-finite values.
Results may differ from a plain program's by a relative error of at most 0.0122927.
Values are sent between devices in bfloat16 or wider.
A program may use at most 1 GiB of HBM per device.

v0:
```python
import math
import jax
import jax.numpy as jnp
from jax import lax
from jax.sharding import PartitionSpec as P

HEAD_DIM = 128
LN_EPS = 1e-5
ROPE_BASE = 10000.0


def norm_f32(hid_f32, weight_f32):
    mean_val = jnp.mean(hid_f32, axis=-1, keepdims=True)
    centered = hid_f32 - mean_val
    var_val = jnp.mean(centered * centered, axis=-1, keepdims=True)
    return centered * lax.rsqrt(var_val + LN_EPS) * weight_f32


def rope_tables(positions):
    inv_freq = ROPE_BASE ** (-jnp.arange(0, HEAD_DIM, 2, dtype=jnp.float32) / HEAD_DIM)
    angles = positions.astype(jnp.float32)[:, None] * inv_freq[None, :]
    return jnp.cos(angles)[:, None, :], jnp.sin(angles)[:, None, :]


def apply_rope(values, cos_t, sin_t):
    rot_pairs = values.reshape(values.shape[:-1] + (HEAD_DIM // 2, 2))
    even_part = rot_pairs[..., 0]
    odd_part = rot_pairs[..., 1]
    new_even = even_part * cos_t - odd_part * sin_t
    new_odd = odd_part * cos_t + even_part * sin_t
    return jnp.stack([new_even, new_odd], axis=-1).reshape(values.shape)


def block_probs(q_block, row_start, k_all):
    scores = jnp.einsum('qgrd,kgd->grqk', q_block, k_all, preferred_element_type=jnp.float32) * (HEAD_DIM ** -0.5)
    row_ids = row_start + jnp.arange(q_block.shape[0])
    col_ids = jnp.arange(k_all.shape[0])
    scores = jnp.where(row_ids[:, None] >= col_ids[None, :], scores, -jnp.inf)
    return jax.nn.softmax(scores, axis=-1)


def attn_forward(q_grp, k_all, v_all, row_offset):
    n_rows = q_grp.shape[0]
    block_rows = math.gcd(n_rows, 128)
    q_blocks = q_grp.reshape((n_rows // block_rows, block_rows) + q_grp.shape[1:])

    def one_block(block_in):
        q_block, block_idx = block_in
        attn_prob = block_probs(q_block, row_offset + block_idx * block_rows, k_all)
        return jnp.einsum('grqk,kgd->qgrd', attn_prob.astype(jnp.bfloat16), v_all, preferred_element_type=jnp.float32).astype(jnp.bfloat16)

    o_blocks = lax.map(one_block, (q_blocks, jnp.arange(n_rows // block_rows)))
    return o_blocks.reshape(q_grp.shape)


def attn_backward(q_grp, k_all, v_all, do_grp, row_offset):
    n_rows = q_grp.shape[0]
    block_rows = math.gcd(n_rows, 128)
    block_shape = (n_rows // block_rows, block_rows) + q_grp.shape[1:]

    def one_block(carry, block_in):
        dk_acc, dv_acc = carry
        q_block, do_block, block_idx = block_in
        attn_prob = block_probs(q_block, row_offset + block_idx * block_rows, k_all)
        d_prob = jnp.einsum('qgrd,kgd->grqk', do_block, v_all, preferred_element_type=jnp.float32)
        row_dot = jnp.sum(attn_prob * d_prob, axis=-1, keepdims=True)
        d_score = (attn_prob * (d_prob - row_dot) * (HEAD_DIM ** -0.5)).astype(jnp.bfloat16)
        dq_block = jnp.einsum('grqk,kgd->qgrd', d_score, k_all, preferred_element_type=jnp.float32).astype(jnp.bfloat16)
        dk_acc = dk_acc + jnp.einsum('grqk,qgrd->kgd', d_score, q_block, preferred_element_type=jnp.float32)
        dv_acc = dv_acc + jnp.einsum('grqk,qgrd->kgd', attn_prob.astype(jnp.bfloat16), do_block, preferred_element_type=jnp.float32)
        return (dk_acc, dv_acc), dq_block

    zero_acc = jnp.zeros(k_all.shape, jnp.float32)
    kv_sums, dq_blocks = lax.scan(one_block, (zero_acc, zero_acc), (q_grp.reshape(block_shape), do_grp.reshape(block_shape), jnp.arange(block_shape[0])))
    return dq_blocks.reshape(q_grp.shape), kv_sums[0], kv_sums[1]


def solution(mesh):
    sp_size = mesh.shape['sp']
    row_spec = P(('dp', 'sp'), None)
    pos_spec = P(('dp', 'sp'))
    full_spec = P(None, None)
    grad_spec = P('dp', None)

    def local_step(hidden, positions, d_attn, ln_weight, w_q, w_k, w_v, w_o):
        local_rows = hidden.shape[0]
        n_heads = w_q.shape[1] // HEAD_DIM
        kv_heads = w_k.shape[1] // HEAD_DIM
        copies = max(sp_size // kv_heads, 1)
        normed32, norm_vjp = jax.vjp(norm_f32, hidden.astype(jnp.float32), ln_weight.astype(jnp.float32))
        normed = normed32.astype(jnp.bfloat16)
        cos_t, sin_t = rope_tables(positions)
        q_rot = apply_rope(jnp.dot(normed, w_q, preferred_element_type=jnp.float32).reshape(local_rows, n_heads, HEAD_DIM), cos_t, sin_t).astype(jnp.bfloat16)
        k_rot = apply_rope(jnp.dot(normed, w_k, preferred_element_type=jnp.float32).reshape(local_rows, kv_heads, HEAD_DIM), cos_t, sin_t).astype(jnp.bfloat16)
        v_loc = jnp.dot(normed, w_v, preferred_element_type=jnp.float32).astype(jnp.bfloat16).reshape(local_rows, kv_heads, HEAD_DIM)
        if copies > 1:
            k_rot = jnp.repeat(k_rot, copies, axis=1)
            v_loc = jnp.repeat(v_loc, copies, axis=1)
        q_heads = lax.all_to_all(q_rot, 'sp', 1, 0, tiled=True)
        k_heads = lax.all_to_all(k_rot, 'sp', 1, 0, tiled=True)
        v_heads = lax.all_to_all(v_loc, 'sp', 1, 0, tiled=True)
        seq_rows, heads_local = q_heads.shape[0], q_heads.shape[1]
        kv_local = k_heads.shape[1]
        q_grp = q_heads.reshape(seq_rows, kv_local, heads_local // kv_local, HEAD_DIM)
        o_grp = attn_forward(q_grp, k_heads, v_heads, 0)
        o_tok = lax.all_to_all(o_grp.reshape(q_heads.shape), 'sp', 0, 1, tiled=True).reshape(local_rows, n_heads * HEAD_DIM)
        attn_out = jnp.dot(o_tok, w_o, preferred_element_type=jnp.float32).astype(jnp.bfloat16)
        d_o = jnp.einsum('td,ed->te', d_attn, w_o, preferred_element_type=jnp.float32).astype(jnp.bfloat16)
        dw_o = jnp.einsum('te,td->ed', o_tok, d_attn, preferred_element_type=jnp.float32)
        do_heads = lax.all_to_all(d_o.reshape(local_rows, n_heads, HEAD_DIM), 'sp', 1, 0, tiled=True)
        dq_grp, dk_acc, dv_acc = attn_backward(q_grp, k_heads, v_heads, do_heads.reshape(q_grp.shape), 0)
        dq_tok = lax.all_to_all(dq_grp.reshape(q_heads.shape), 'sp', 0, 1, tiled=True)
        dk_tok = lax.all_to_all(dk_acc.astype(jnp.bfloat16), 'sp', 0, 1, tiled=True)
        dv_tok = lax.all_to_all(dv_acc.astype(jnp.bfloat16), 'sp', 0, 1, tiled=True)
        if copies > 1:
            dk_tok = dk_tok.reshape(local_rows, kv_heads, copies, HEAD_DIM).astype(jnp.float32).sum(axis=2).astype(jnp.bfloat16)
            dv_tok = dv_tok.reshape(local_rows, kv_heads, copies, HEAD_DIM).astype(jnp.float32).sum(axis=2).astype(jnp.bfloat16)
        g_q = apply_rope(dq_tok.astype(jnp.float32), cos_t, -sin_t).astype(jnp.bfloat16).reshape(local_rows, n_heads * HEAD_DIM)
        g_k = apply_rope(dk_tok.astype(jnp.float32), cos_t, -sin_t).astype(jnp.bfloat16).reshape(local_rows, kv_heads * HEAD_DIM)
        g_v = dv_tok.reshape(local_rows, kv_heads * HEAD_DIM)
        d_normed = (jnp.einsum('te,de->td', g_q, w_q, preferred_element_type=jnp.float32)
                    + jnp.einsum('te,de->td', g_k, w_k, preferred_element_type=jnp.float32)
                    + jnp.einsum('te,de->td', g_v, w_v, preferred_element_type=jnp.float32))
        dw_q = jnp.einsum('td,te->de', normed, g_q, preferred_element_type=jnp.float32)
        dw_k = jnp.einsum('td,te->de', normed, g_k, preferred_element_type=jnp.float32)
        dw_v = jnp.einsum('td,te->de', normed, g_v, preferred_element_type=jnp.float32)
        d_hid, d_lnw = norm_vjp(d_normed)
        grad_sums = lax.psum((d_lnw, dw_q, dw_k, dw_v, dw_o), 'sp')
        return (attn_out, d_hid.astype(jnp.bfloat16), grad_sums[0].astype(jnp.bfloat16), grad_sums[1].astype(jnp.bfloat16),
                grad_sums[2].astype(jnp.bfloat16), grad_sums[3].astype(jnp.bfloat16), grad_sums[4].astype(jnp.bfloat16))

    return jax.shard_map(local_step, mesh=mesh,
                         in_specs=(row_spec, pos_spec, row_spec, P(None), full_spec, full_spec, full_spec, full_spec),
                         out_specs=(row_spec, row_spec, P('dp'), grad_spec, grad_spec, grad_spec, grad_spec),
                         check_vma=False)
```

profile of v0, /device:TPU:0, one launch (start us, length us, event | category | flops | bytes accessed | tf_op | source)
XLA Modules:
  0.0 3270.2 jit_solution(17931634778781306045)
XLA Ops:
  8.3 8.9 fusion.82
  38.8 19.4 fusion.71
  65.1 22.9 fusion.84
  88.0 12.0 reshape_reshape.19
  100.0 15.0 subtract_convert_fusion.1
  115.0 11.3 pad_maximum_fusion
  138.0 8.7 fusion.72
  148.1 44.5 %all-to-all-done = bf16[768,24,128]{0,2,1:T(8,128)(2,1)} async-done(((bf16[768,24,128]{0,2,1:T(8,128)(2,1)}), bf16[768,24,128]{0,2,1:T(8,128)(2,1)}, u32[]{:S(2)}, u32[]{:S(2)}) %all-to-all-start) | async-done | bytes 4718624 | tf_op jit(solution)/shard_map/all_to_all | solution.py:99
  201.5 6.6 copy.131
  208.1 6.4 copy.137
  219.9 1069.2 %while.26 = (s32[]{:T(128)}, f32[6144,1,128]{0,2,1:T(8,128)}, f32[6144,1,128]{0,2,1:T(8,128)}, bf16[48,128,1,3,128]{4,1,0,3,2:T(8,128)(2,1)}, bf16[48,128,1,3,12...) while((s32[]{:T(128)}, f32[6144,1,128]{0,2,1:T(8,128)}, ...), condition=%wide.region_10.11_spmd.clone, body=%wide.region_6.10_spmd.clone.sunk | while | flops 3066346496 | bytes 124765944 | solution.py:74
  1303.9 462.8 %while.25 = (s32[]{:T(128)}, bf16[48,128,1,3,128]{4,1,0,3,2:T(8,128)(2,1)}, s32[48]{0:T(128)S(1)}, bf16[48,128,1,3,128]{4,1,3,2,0:T(8,128)(2,1)}, bf16[6144,1,12...) while((s32[]{:T(128)}, bf16[48,128,1,3,128]{4,1,0,3,2:T(8,128)(2,1)}, ...), condition=%wide.region_5.6_spmd, body=%wide.region_2.5_spmd.sunk | while | flops 1227668864 | bytes 33235584 | solution.py:52
  1766.7 9.3 copy.147
  1784.3 9.3 copy.139
  1830.3 10.9 fusion.77
  1841.3 8.8 fusion.75
  1850.0 7.6 fusion.91
  1857.6 7.5 fusion.90
  1865.1 28.8 all-to-all-done.3
  1903.3 6.7 copy.141
  1909.9 20.8 convolution_convert_fusion.1
  1930.8 19.5 fusion.92
  1950.3 18.8 all-to-all-done.5
  1977.2 9.6 copy.149
  1986.8 12.0 reshape.249
  1998.8 15.9 subtract_convert_fusion
  2014.7 11.7 pad_maximum_fusion.1
  2026.4 10.8 convert_element_type.135
  2037.2 24.0 fusion.79
  2061.2 26.8 fusion.68
  2088.1 6.5 fusion.86
  2098.4 1171.6 %all-reduce.2 = (bf16[3072]{0:T(1024)(128)(2,1)}, bf16[3072,3072]{1,0:T(8,128)(2,1)}, bf16[3072,1024]{1,0:T(8,128)(2,1)}, bf16[3072,1024]{1,0:T(8,128)(2,1)}, bf16[3072,3072]{1,0:T(8,128)(2,1)}) all-reduce(f32[3072]{0:T(1024)S(1)} %get-tuple-element.197, f32[3072,3072]{1,0:T(8,128)} %fusion.79, ...), channel_id=1, replica_groups=mesh['dp'=1,'sp'=8] {'sp'}, use_global_device_ids=true, to_apply=%region_14.15 | all-reduce | flops 25168896 | bytes 151013376 | tf_op jit(solution)/shard_map/psum | solution.py:128
  (1077 shorter events, 1609.9 us)
Async XLA Ops:
  0.6 5.1 copy-start.2
  2.7 5.0 copy-start.18
  5.8 132.2 %copy-start.13 = (f32[768]{0:T(1024)}, f32[768]{0:T(1024)S(1)}, u32[]{:S(2)}) copy-start(f32[768]{0:T(1024)S(1)} %broadcast_multiply_fusion) | copy-start | bytes 9220
  8.3 129.6 %copy-start.9 = (f32[3072]{0:T(1024)}, f32[3072]{0:T(1024)S(1)}, u32[]{:S(2)}) copy-start(f32[3072]{0:T(1024)S(1)} %convert_element_type.123) | copy-start | bytes 36868
  23.2 76.8 %copy-start.4 = (f32[768,64]{0,1:T(8,128)}, f32[768,64]{0,1:T(8,128)S(1)}, u32[]{:S(2)}) copy-start(f32[768,64]{0,1:T(8,128)S(1)} %get-tuple-element.254) | copy-start | bytes 589828
  34.3 27.4 all-to-all-start.1
  61.6 3.5 copy-start.16
  61.6 72.9 %all-to-all-start.4 = ((bf16[768,24,128]{2,0,1:T(8,128)(2,1)}), bf16[768,24,128]{2,0,1:T(8,128)(2,1)}, u32[]{:S(2)}, u32[]{:S(2)}) async-start(bf16[768,24,128]{2,0,1:T(8,128)(2,1)} %bitcast.270), calls=%async_computation.4 | async-start | bytes 9437184 | tf_op jit(solution)/shard_map/all_to_all | solution.py:110
  134.6 58.0 %all-to-all-start = ((bf16[768,24,128]{0,2,1:T(8,128)(2,1)}), bf16[768,24,128]{0,2,1:T(8,128)(2,1)}, u32[]{:S(2)}, u32[]{:S(2)}) async-start(bf16[768,24,128]{0,2,1:T(8,128)(2,1)} %copy.129), calls=%async_computation | async-start | bytes 9437184 | tf_op jit(solution)/shard_map/all_to_all | solution.py:99
  192.6 23.9 all-to-all-start.2
  234.1 3.2 copy-start
  278.7 3.2 copy-start
  300.9 3.2 copy-start
  323.2 3.2 copy-start
  345.5 3.2 copy-start
  367.8 3.2 copy-start
  1298.2 495.4 %all-to-all-start.6 = ((bf16[8,2,49152]{2,1,0:T(2,128)(2,1)}), bf16[8,2,49152]{2,1,0:T(2,128)(2,1)S(1)}, u32[]{:S(2)}, u32[]{:S(2)}) async-start(bf16[8,2,49152]{2,1,0:T(2,128)(2,1)} %reshape.267), calls=%async_computation.6 | async-start | bytes 3145728 | tf_op jit(solution)/shard_map/all_to_all | solution.py:113
  1794.8 23.9 all-to-all-start.7
  1818.7 75.2 %all-to-all-start.3 = ((bf16[6144,3,128]{2,1,0:T(4,128)(2,1)}), bf16[6144,3,128]{2,1,0:T(4,128)(2,1)}, u32[]{:S(2)}, u32[]{:S(2)}) async-start(bf16[6144,3,128]{2,1,0:T(4,128)(2,1)} %copy.139), calls=%async_computation.3 | async-start | bytes 12582912 | tf_op jit(solution)/shard_map/all_to_all | solution.py:106
  1828.5 12.7 slice-start
  1830.3 11.0 slice-start.1
  1830.3 10.9 copy-start.17
  1830.3 19.7 slice-start.2
  1830.3 27.3 slice-start.4
  1841.2 8.8 slice-start.3
  1841.2 16.4 slice-start.5
  1850.0 7.6 copy-start.8
  1893.9 75.2 %all-to-all-start.5 = ((bf16[6144,3,128]{2,1,0:T(4,128)(2,1)}), bf16[6144,3,128]{2,1,0:T(4,128)(2,1)}, u32[]{:S(2)}, u32[]{:S(2)}) async-start(bf16[6144,3,128]{2,1,0:T(4,128)(2,1)} %copy.147), calls=%async_computation.5 | async-start | bytes 12582912 | tf_op jit(solution)/shard_map/all_to_all | solution.py:112
  1903.3 27.5 slice-start.6
  1909.9 20.8 copy-start.6
  1909.9 20.8 slice-start.7
  2061.2 26.9 copy-start.12
  (97 other events, 245.1 us)
where the time goes:
time: 3290 us; the launch traced here: 3270 us
  matrix products  1260 us (38%)
  blocking collectives  1170 us (36%)
  other arithmetic  438 us (13%)
  local copies, waits for them, and re-layouts  209 us (6%)
  waiting for transfers between devices  98 us (3%)
  loops' own time  66.4 us (2%)
    psum x1, blocking collectives, local_step(): grad_sums = lax.psum((d_lnw, dw_q, dw_k, dw_v, dw_o), 'sp')  1170 us
    dot_general x96, matrix products, block_probs(): jnp.einsum('qgrd,kgd->grqk', q_block, k_all, preferred_element_type=jnp.f...  270 us
    dot_general x48, matrix products, one_block(): jnp.einsum('grqk,qgrd->kgd', attn_prob.astype(jnp.bfloat16), do_block, pr...  229 us
    another operation x52, other arithmetic  189 us
    dot_general x48, matrix products, one_block(): jnp.einsum('qgrd,kgd->grqk', do_block, v_all, preferred_element_type=jnp....  181 us
    dot_general x48, matrix products, one_block(): jnp.einsum('grqk,kgd->qgrd', attn_prob.astype(jnp.bfloat16), v_all, prefe...  175 us
    reduce_sum x96, other arithmetic, block_probs(): return jax.nn.softmax(scores, axis=-1)  136 us
    dot_general x48, matrix products, one_block(): jnp.einsum('grqk,qgrd->kgd', d_score, q_block, preferred_element_type=jnp...  119 us
  transfers between devices with their start and end apart: 8, of which 5 were waited for; matrix products, arithmetic and copies ran while one was open for 21% of the time, Pallas kernels for 0%

commit v1 on v0

v1 whole, which is shorter than its diff:
```python
import functools
import math
import jax
import jax.numpy as jnp
from jax import lax
from jax.experimental import pallas as pl
from jax.experimental.pallas import tpu as pltpu
from jax.sharding import PartitionSpec as P

D = 128
LN_EPS = 1e-5
ROPE_BASE = 10000.0
SCALE = D ** -0.5
SCALE2 = SCALE * math.log2(math.e)
NT = (((1,), (1,)), ((), ()))
f32 = jnp.float32
bf16 = jnp.bfloat16
VMEM_LIMIT = 60 * 2 ** 20


def rotate(val, cos, sin):
    even = lax.rem(lax.broadcasted_iota(jnp.int32, val.shape, 1), 2) == 0
    swapped = jnp.where(even, pltpu.roll(val, D - 1, 1), pltpu.roll(val, 1, 1))
    return val * cos + swapped * sin


def proj_kernel(h_ref, w_ref, cos_ref, sin_ref, q_ref, qt_ref, k_ref, v_ref, vt_ref, *, nh):
    h = h_ref[...]
    cos, sin = cos_ref[...], sin_ref[...]
    res = jnp.dot(h, w_ref[...], preferred_element_type=f32)
    for n in range(nh):
        rot = rotate(res[:, n * D:(n + 1) * D], cos, sin).astype(bf16)
        q_ref[:, n * D:(n + 1) * D] = rot
        qt_ref[n * D:(n + 1) * D, :] = rot.T
    k_ref[...] = rotate(res[:, nh * D:(nh + 1) * D], cos, sin).astype(bf16)
    v = res[:, (nh + 1) * D:].astype(bf16)
    v_ref[...] = v
    vt_ref[...] = v.T


def project(h, w, cos, sin, nh, bt=512):
    t, d = h.shape
    row = lambda c: pl.BlockSpec((bt, c), lambda i: (i, 0))
    col = lambda r: pl.BlockSpec((r, bt), lambda i: (0, i))
    return pl.pallas_call(
        functools.partial(proj_kernel, nh=nh),
        grid=(t // bt,),
        in_specs=[row(d), pl.BlockSpec((d, w.shape[1]), lambda i: (0, 0)), row(D), row(D)],
        out_specs=[row(nh * D), col(nh * D), row(D), row(D), col(D)],
        out_shape=[jax.ShapeDtypeStruct((t, nh * D), bf16), jax.ShapeDtypeStruct((nh * D, t), bf16),
                   jax.ShapeDtypeStruct((t, D), bf16), jax.ShapeDtypeStruct((t, D), bf16), jax.ShapeDtypeStruct((D, t), bf16)],
        compiler_params=pltpu.CompilerParams(vmem_limit_bytes=VMEM_LIMIT, dimension_semantics=("arbitrary",)),
        cost_estimate=pl.CostEstimate(flops=2 * t * d * w.shape[1], bytes_accessed=2 * t * d, transcendentals=0),
        name="qkv_proj")(h, w, cos, sin)


def dout_kernel(g_ref, w_ref, do_ref, dot_ref):
    val = lax.dot_general(g_ref[...], w_ref[...], NT, preferred_element_type=f32).astype(bf16)
    do_ref[...] = val
    dot_ref[...] = val.T


def dout_proj(g, w, bt=512):
    t, d = g.shape
    e = w.shape[0]
    return pl.pallas_call(
        dout_kernel,
        grid=(t // bt,),
        in_specs=[pl.BlockSpec((bt, d), lambda i: (i, 0)), pl.BlockSpec((e, d), lambda i: (0, 0))],
        out_specs=[pl.BlockSpec((bt, e), lambda i: (i, 0)), pl.BlockSpec((e, bt), lambda i: (0, i))],
        out_shape=[jax.ShapeDtypeStruct((t, e), bf16), jax.ShapeDtypeStruct((e, t), bf16)],
        compiler_params=pltpu.CompilerParams(vmem_limit_bytes=VMEM_LIMIT, dimension_semantics=("arbitrary",)),
        cost_estimate=pl.CostEstimate(flops=2 * t * d * e, bytes_accessed=2 * t * d, transcendentals=0),
        name="dout_proj")(g, w)


def fwd_kernel(q_ref, k_ref, vt_ref, o_ref, lse_ref, acc, ml, *, bq, bk, nh):
    i = pl.program_id(0)
    for h in range(nh):
        ml[2 * h:2 * h + 1, :] = jnp.full((1, bq), -1e30, f32)
        ml[2 * h + 1:2 * h + 2, :] = jnp.zeros((1, bq), f32)
    acc[...] = jnp.zeros_like(acc)

    def step(off, diag):
        kb = k_ref[pl.ds(off, bk), :]
        vt = vt_ref[:, pl.ds(off, bk)]
        if diag is not None:
            ki = lax.broadcasted_iota(jnp.int32, (bk, bq), 0) + diag
            qi = lax.broadcasted_iota(jnp.int32, (bk, bq), 1)
            keep = ki <= qi
        ss = [lax.dot_general(kb, q_ref[:, h * D:(h + 1) * D], NT, preferred_element_type=f32) for h in range(nh)]
        for h in range(nh):
            s = ss[h]
            if diag is not None:
                s = jnp.where(keep, s, -1e30)
            m_old = ml[2 * h:2 * h + 1, :]
            m_new = jnp.maximum(m_old, jnp.max(s, axis=0, keepdims=True))
            p = jnp.exp2(s * SCALE2 - m_new * SCALE2)
            alpha = jnp.exp2((m_old - m_new) * SCALE2)
            ml[2 * h:2 * h + 1, :] = m_new
            ml[2 * h + 1:2 * h + 2, :] = ml[2 * h + 1:2 * h + 2, :] * alpha + jnp.sum(p, axis=0, keepdims=True)
            pv = jnp.dot(vt, p.astype(bf16), preferred_element_type=f32)
            acc[h * D:(h + 1) * D, :] = acc[h * D:(h + 1) * D, :] * alpha + pv

    ratio = bq // bk

    def body(j, carry):
        step(pl.multiple_of(j * bk, bk), None)
        return carry

    lax.fori_loop(0, i * ratio, body, 0)
    for d in range(ratio):
        step(pl.multiple_of(i * bq + d * bk, bk), d * bk)
    for h in range(nh):
        m = ml[2 * h:2 * h + 1, :]
        l = ml[2 * h + 1:2 * h + 2, :]
        out_t = acc[h * D:(h + 1) * D, :] * (1.0 / l)
        o_ref[:, h * D:(h + 1) * D] = out_t.T.astype(bf16)
        lse_ref[:, h * D:(h + 1) * D] = jnp.broadcast_to(m * SCALE2 + jnp.log2(l), (D, bq)).T


def attn_fwd(q, k, vt, bq=1024, bk=512):
    t, e = q.shape
    nh = e // D
    row = pl.BlockSpec((bq, e), lambda i: (i, 0))
    return pl.pallas_call(
        functools.partial(fwd_kernel, bq=bq, bk=bk, nh=nh),
        grid=(t // bq,),
        in_specs=[row, pl.BlockSpec((t, D), lambda i: (0, 0)), pl.BlockSpec((D, t), lambda i: (0, 0))],
        out_specs=[row, row],
        out_shape=[jax.ShapeDtypeStruct((t, e), bf16), jax.ShapeDtypeStruct((t, e), f32)],
        scratch_shapes=[pltpu.VMEM((e, bq), f32), pltpu.VMEM((8, bq), f32)],
        compiler_params=pltpu.CompilerParams(vmem_limit_bytes=VMEM_LIMIT, dimension_semantics=("arbitrary",)),
        cost_estimate=pl.CostEstimate(flops=4 * t * t * e, bytes_accessed=8 * t * e, transcendentals=0),
        name="attn_fwd")(q, k, vt)


def bwd_kernel(q_ref, qt_ref, do_ref, dot_ref, o_ref, lse_ref, k_ref, v_ref, cos_ref, sin_ref,
               dq_ref, dk_ref, dv_ref, dlt, dqa, dka, dva, *, bq, bk, t, nh):
    h = pl.program_id(0)
    j = pl.program_id(1)
    nq = t // bq
    rep = bk // D
    koff = pl.multiple_of(j * bk, bk)
    kc = pl.ds(koff, bk)

    @pl.when(j == 0)
    def _():
        def init(i, carry):
            r = pl.ds(pl.multiple_of(i * bq, bq), bq)
            d = jnp.sum(do_ref[r, :].astype(f32) * o_ref[r, :].astype(f32), axis=1, keepdims=True)
            dlt[r, :] = jnp.broadcast_to(d, (bq, D))
            dqa[r, :] = jnp.zeros((bq, D), f32)
            return carry
        lax.fori_loop(0, nq, init, 0)

    @pl.when(h == 0)
    def _():
        dka[:, kc] = jnp.zeros((D, bk), f32)
        dva[:, kc] = jnp.zeros((D, bk), f32)

    kb = k_ref[...]
    vb = v_ref[...]

    def step(i, diag):
        off = pl.multiple_of(i * bq, bq)
        r = pl.ds(off, bq)
        s = lax.dot_general(q_ref[r, :], kb, NT, preferred_element_type=f32)
        dp = lax.dot_general(do_ref[r, :], vb, NT, preferred_element_type=f32)
        if diag:
            qi = lax.broadcasted_iota(jnp.int32, (bq, bk), 0) + (off - koff)
            ki = lax.broadcasted_iota(jnp.int32, (bq, bk), 1)
            s = jnp.where(ki <= qi, s, -1e30)
        p = jnp.exp2(s * SCALE2 - jnp.concatenate([lse_ref[r, :]] * rep, axis=1))
        ds = ((dp - jnp.concatenate([dlt[r, :]] * rep, axis=1)) * p * SCALE).astype(bf16)
        dva[:, kc] += jnp.dot(dot_ref[:, r], p.astype(bf16), preferred_element_type=f32)
        dka[:, kc] += jnp.dot(qt_ref[:, r], ds, preferred_element_type=f32)
        dqa[r, :] += jnp.dot(ds, kb, preferred_element_type=f32)

    ratio = max(bk // bq, 1)
    first = (j * bk) // bq
    for d in range(ratio):
        step(first + d, True)

    def body(i, carry):
        step(i, False)
        return carry

    lax.fori_loop(first + ratio, nq, body, 0)

    @pl.when(j == pl.num_programs(1) - 1)
    def _():
        def fin(i, carry):
            r = pl.ds(pl.multiple_of(i * bq, bq), bq)
            dq = dqa[r, :].astype(bf16).astype(f32)
            dq_ref[r, :] = rotate(dq, cos_ref[r, :], -sin_ref[r, :]).astype(bf16)
            return carry
        lax.fori_loop(0, nq, fin, 0)

    @pl.when(h == nh - 1)
    def _():
        dk = dka[:, kc].T.astype(bf16).astype(f32)
        dk_ref[...] = rotate(dk, cos_ref[kc, :], -sin_ref[kc, :]).astype(bf16)
        dv_ref[...] = dva[:, kc].T.astype(bf16)


def attn_bwd(q, qt, do, dot, o, lse, k, v, cos, sin, bq=512, bk=1024):
    t, e = q.shape
    nh = e // D
    col = pl.BlockSpec((t, D), lambda h, j: (0, h))
    row_t = pl.BlockSpec((D, t), lambda h, j: (h, 0))
    kv_in = pl.BlockSpec((bk, D), lambda h, j: (j, 0))
    kv_out = pl.BlockSpec((bk, D), lambda h, j: (jnp.where(h == nh - 1, j, 0), 0))
    table = pl.BlockSpec((t, D), lambda h, j: (0, 0), pipeline_mode=pl.Buffered(1))
    return pl.pallas_call(
        functools.partial(bwd_kernel, bq=bq, bk=bk, t=t, nh=nh),
        grid=(nh, t // bk),
        in_specs=[col, row_t, col, row_t, col, col, kv_in, kv_in, table, table],
        out_specs=[col, kv_out, kv_out],
        out_shape=[jax.ShapeDtypeStruct((t, e), bf16), jax.ShapeDtypeStruct((t, D), bf16), jax.ShapeDtypeStruct((t, D), bf16)],
        scratch_shapes=[pltpu.VMEM((t, D), f32), pltpu.VMEM((t, D), f32), pltpu.VMEM((D, t), f32), pltpu.VMEM((D, t), f32)],
        compiler_params=pltpu.CompilerParams(vmem_limit_bytes=VMEM_LIMIT, dimension_semantics=("arbitrary", "arbitrary")),
        cost_estimate=pl.CostEstimate(flops=10 * t * t * e, bytes_accessed=20 * t * e, transcendentals=0),
        name="attn_bwd")(q, qt, do, dot, o, lse, k, v, cos, sin)


def norm_f32(hid_f32, weight_f32):
    mean_val = jnp.mean(hid_f32, axis=-1, keepdims=True)
    centered = hid_f32 - mean_val
    var_val = jnp.mean(centered * centered, axis=-1, keepdims=True)
    return centered * lax.rsqrt(var_val + LN_EPS) * weight_f32


def rope_tables(positions):
    lane = jnp.arange(D, dtype=jnp.int32)
    inv_freq = ROPE_BASE ** (-(lane - lane % 2).astype(f32) / D)
    angles = positions.astype(f32)[:, None] * inv_freq[None, :]
    sin = jnp.sin(angles)
    return jnp.cos(angles), jnp.where(lane[None, :] % 2 == 0, -sin, sin)


def solution(mesh):
    n_dev = mesh.shape['sp']
    row_spec = P(('dp', 'sp'), None)
    pos_spec = P(('dp', 'sp'))
    full_spec = P(None, None)
    grad_spec = P('dp', None)

    def local_step(hidden, positions, d_attn, ln_weight, w_q, w_k, w_v, w_o):
        rows, dim = hidden.shape
        idx = lax.axis_index('sp')
        qe = w_q.shape[1] // n_dev
        ke = w_k.shape[1] // n_dev
        normed32, norm_vjp = jax.vjp(norm_f32, hidden.astype(f32), ln_weight.astype(f32))
        h_all = lax.all_gather(normed32.astype(bf16), 'sp', axis=0, tiled=True)
        g_all = lax.all_gather(d_attn, 'sp', axis=0, tiled=True)
        cos, sin = rope_tables(lax.all_gather(positions, 'sp', axis=0, tiled=True))
        w_own = jnp.concatenate([lax.dynamic_slice_in_dim(w_q, idx * qe, qe, 1), lax.dynamic_slice_in_dim(w_k, idx * ke, ke, 1),
                                 lax.dynamic_slice_in_dim(w_v, idx * ke, ke, 1)], axis=1)
        wo_own = lax.dynamic_slice_in_dim(w_o, idx * qe, qe, 0)
        q, qt, k, v, vt = project(h_all, w_own, cos, sin, qe // D)
        o, lse = attn_fwd(q, k, vt)
        o_tok = lax.all_to_all(o.reshape(n_dev, rows, qe), 'sp', 0, 0)
        attn_out = jnp.einsum('stn,snd->td', o_tok, w_o.reshape(n_dev, qe, dim), preferred_element_type=f32).astype(bf16)
        do, dot = dout_proj(g_all, wo_own)
        dwo_own = jnp.einsum('te,td->ed', o, g_all, preferred_element_type=f32).astype(bf16)
        dw_o = lax.all_gather(dwo_own, 'sp', axis=0, tiled=True)
        gq, gk, gv = attn_bwd(q, qt, do, dot, o, lse, k, v, cos, sin)
        g_own = jnp.concatenate([gq, gk, gv], axis=1)
        g_tok = lax.all_to_all(g_own.reshape(n_dev, rows, qe + 2 * ke), 'sp', 0, 0)
        dw_own = jnp.einsum('te,td->ed', g_own, h_all, preferred_element_type=f32).astype(bf16)
        dw_all = lax.all_gather(dw_own, 'sp', axis=0, tiled=False)
        dw_q = dw_all[:, :qe].reshape(n_dev * qe, dim).T
        dw_k = dw_all[:, qe:qe + ke].reshape(n_dev * ke, dim).T
        dw_v = dw_all[:, qe + ke:].reshape(n_dev * ke, dim).T
        d_normed = (jnp.einsum('ste,dse->td', g_tok[:, :, :qe], w_q.reshape(dim, n_dev, qe), preferred_element_type=f32)
                    + jnp.einsum('ste,dse->td', g_tok[:, :, qe:qe + ke], w_k.reshape(dim, n_dev, ke), preferred_element_type=f32)
                    + jnp.einsum('ste,dse->td', g_tok[:, :, qe + ke:], w_v.reshape(dim, n_dev, ke), preferred_element_type=f32))
        d_hid, d_lnw = norm_vjp(d_normed)
        return (attn_out, d_hid.astype(bf16), lax.psum(d_lnw, 'sp').astype(bf16), dw_q, dw_k, dw_v, dw_o)

    return jax.shard_map(local_step, mesh=mesh,
                         in_specs=(row_spec, pos_spec, row_spec, P(None), full_spec, full_spec, full_spec, full_spec),
                         out_specs=(row_spec, row_spec, P('dp'), grad_spec, grad_spec, grad_spec, grad_spec),
                         check_vma=False)
```

time: 3290 us -> 1110 us (0.34)
  matrix products: 1260 us -> 119 us
  blocking collectives: 1170 us -> 136 us
  other arithmetic: 438 us -> 35.6 us
  Pallas kernels: 0 us -> 364 us
  waiting for transfers between devices: 98 us -> 327 us
  local copies, waits for them, and re-layouts: 209 us -> 102 us
  loops' own time: 66.4 us -> 0 us
    psum x1, blocking collectives: 1170 us -> 22.6 us  [local_step(): lax.psum(d_lnw, 'sp').astype(bf16)]
    dot_general x348 -> x6, matrix products: 1260 us -> 119 us  [the longest x1 30.7 us: local_step(): jnp.einsum('te,td->ed', g_own, h_all, preferred_element_type=f32)]
    pallas_call x0 -> x4, Pallas kernels: none -> 364 us  [the longest x1 194 us: attn_bwd(): pl.pallas_call(functools.partial(bwd_kernel, bq=bq, bk=bk, t=t, nh=nh), g...]
    another operation x56 -> x0, other arithmetic: 220 us -> none
    all_gather x0 -> x4, waiting for transfers between devices: none -> 177 us  [the longest x1 143 us: local_step(): h_all = lax.all_gather(normed32.astype(bf16), 'sp', axis=0, tiled=True)]
    reduce_sum x96 -> x0, other arithmetic: 136 us -> none  [block_probs(): return jax.nn.softmax(scores, axis=-1)]
    all_to_all x0 -> x1, blocking collectives: none -> 99.8 us  [local_step(): o_tok = lax.all_to_all(o.reshape(n_dev, rows, qe), 'sp', 0, 0)]
    another operation x2 -> x0, loops' own time: 66.4 us -> none  [the longest x1 34.2 us: attn_backward(): lax.scan(one_block, (zero_acc, zero_acc), (q_grp.reshape(block_shape), do...]
  transfers between devices with their start and end apart: 8 -> 5, of which waited for: 5 -> 3; matrix products, arithmetic and copies ran while one was open for 21% -> 12% of each run, Pallas kernels for 0% -> 33%
where the time goes in v1:
time: 1110 us; the launch traced here: 1100 us
  Pallas kernels  364 us (33%)
  waiting for transfers between devices  327 us (29%)
  blocking collectives  136 us (12%)
  matrix products  119 us (11%)
  local copies, waits for them, and re-layouts  102 us (9%)
  other arithmetic  35.6 us (3%)
  between operations  14.4 us (1%)
    pallas_call x1, Pallas kernels, attn_bwd(): pl.pallas_call(functools.partial(bwd_kernel, bq=bq, bk=bk, t=t, nh=nh), g...  194 us
    all_to_all x1, waiting for transfers between devices, local_step(): g_tok = lax.all_to_all(g_own.reshape(n_dev, rows, qe + 2 * ke), 'sp', 0, 0)  149 us
    all_gather x1, waiting for transfers between devices, local_step(): h_all = lax.all_gather(normed32.astype(bf16), 'sp', axis=0, tiled=True)  143 us
    pallas_call x1, Pallas kernels, attn_fwd(): pl.pallas_call(functools.partial(fwd_kernel, bq=bq, bk=bk, nh=nh), grid=(...  102 us
    all_to_all x1, blocking collectives, local_step(): o_tok = lax.all_to_all(o.reshape(n_dev, rows, qe), 'sp', 0, 0)  99.8 us
    pallas_call x1, Pallas kernels, project(): pl.pallas_call(functools.partial(proj_kernel, nh=nh), grid=(t // bt,), in...  39.8 us
    all_gather x1, waiting for transfers between devices, local_step(): g_all = lax.all_gather(d_attn, 'sp', axis=0, tiled=True)  33.9 us
    dot_general x1, matrix products, local_step(): jnp.einsum('te,td->ed', g_own, h_all, preferred_element_type=f32)  30.7 us
  transfers between devices with their start and end apart: 5, of which 3 were waited for; matrix products, arithmetic and copies ran while one was open for 12% of the time, Pallas kernels for 33%

profile of v1, /device:TPU:0, one launch (start us, length us, event | category | flops | bytes accessed | tf_op | source)
XLA Modules:
  0.0 1101.5 jit_solution(9124423107994148789)
XLA Ops:
  7.2 3.2 convert_reduce_fusion
  14.1 4.6 fusion.9
  19.6 14.1 %all-gather.1 = s32[8,1,768]{2,1,0:T(1,128)S(1)} all-gather(s32[1,1,768]{2,1,0:T(1,128)S(1)} %reshape.105), channel_id=1, replica_groups=mesh['dp'=1,'sp'=8] {'sp'}, dimensions={0}, use_global_device_ids=true | all-gather | bytes 27648 | tf_op jit(solution)/shard_map/all_gather | solution.py:257
  37.2 2.1 pad_maximum_fusion.w_ref
  39.3 13.7 %negate_select_fusion = (f32[6144,128]{1,0:T(8,128)}, f32[6144,128]{1,0:T(8,128)}) fusion(f32[128]{0:T(128)S(1)} %fusion.28, f32[6144]{0:T(1024)S(1)} %bitcast.61, pred[128]{0:T(512)(128)(4,1)S(1)} %broadcast_compare_fusion), kind=kLoop, calls=%fused_computation.27 | loop fusion | flops 2359296 | bytes 6316672 | tf_op jit(solution)/shard_map/jit(_where)/select_n | solution.py:239
  53.1 142.7 %all-gather.7.cloned.1.call-done.h_ref = bf16[6144,3072]{1,0:T(8,128)(2,1)} async-done(((bf16[768,3072]{1,0:T(8,128)(2,1)}), bf16[6144,3072]{1,0:T(8,128)(2,1)}) %all-gather.7.cloned.1.call-update) | async-done | bytes 37748752 | tf_op jit(solution)/shard_map/all_gather | solution.py:255
  195.8 39.8 %qkv_proj.1 = (bf16[6144,384]{1,0:T(8,128)(2,1)}, bf16[384,6144]{1,0:T(8,128)(2,1)}, bf16[6144,128]{1,0:T(8,128)(2,1)}, bf16[6144,128]{1,0:T(8,128)(2,1)}, bf16[128,6144]{1,0:T(8,128)(2,1)}) custom-call(bf16[6144,3072]{1,0:T(8,128)(2,1)} %all-gather.7.cloned.1.call-done.h_ref, bf16[3072,640]{1,0:T(8,128)(2,1)} %pad_maximum_fusion.w_ref, ...), custom_call_target="tpu_custom_call" | custom-call | flops 24159191040 | bytes 37748736 | tf_op jit(solution)/shard_map/qkv_proj/pallas_call | solution.py:45
  235.6 102.1 %attn_fwd.1 = (bf16[6144,384]{1,0:T(8,128)(2,1)}, f32[6144,384]{1,0:T(8,128)}) custom-call(bf16[6144,384]{1,0:T(8,128)(2,1)} %get-tuple-element.19.q_ref, bf16[6144,128]{1,0:T(8,128)(2,1)} %get-tuple-element.20.k_ref, bf16[128,6144]{1,0:T(8,128)(2,1)} %get-tuple-element.21.vt_ref), custom_call_target="tpu_custom_call" | custom-call | flops 57982058496 | bytes 18874368 | tf_op jit(solution)/shard_map/attn_fwd/pallas_call | solution.py:126
  337.7 33.9 %all-gather.9.cloned.1.call-done.g_ref = bf16[6144,3072]{1,0:T(8,128)(2,1)} async-done(((bf16[768,3072]{1,0:T(8,128)(2,1)}), bf16[6144,3072]{1,0:T(8,128)(2,1)}) %all-gather.9.cloned.1.call-update) | async-done | bytes 37748752 | tf_op jit(solution)/shard_map/all_gather | solution.py:256
  371.6 22.2 %convolution_convert_fusion.1 = bf16[384,3072]{1,0:T(8,128)(2,1)} fusion(bf16[6144,384]{1,0:T(8,128)(2,1)} %get-tuple-element.22.o_ref, bf16[6144,3072]{1,0:T(8,128)(2,1)} %all-gather.9.cloned.1.call-done.g_ref), kind=kOutput, calls=%fused_computation.31 | convolution fusion | flops 14496694272 | bytes 44826624 | tf_op jit(solution)/shard_map/te,td->ed/dot_general | solution.py:266
  393.9 3.2 constant_dynamic-slice_fusion.w_ref
  397.1 27.4 %dout_proj.1 = (bf16[6144,384]{1,0:T(8,128)(2,1)}, bf16[384,6144]{1,0:T(8,128)(2,1)}) custom-call(bf16[6144,3072]{1,0:T(8,128)(2,1)} %all-gather.9.cloned.1.call-done.g_ref, bf16[384,3072]{1,0:T(8,128)(2,1)} %constant_dynamic-slice_fusion.w_ref), custom_call_target="tpu_custom_call" | custom-call | flops 14495514624 | bytes 37748736 | tf_op jit(solution)/shard_map/dout_proj/pallas_call | solution.py:66
  424.5 194.3 %attn_bwd.1 = (bf16[6144,384]{1,0:T(8,128)(2,1)}, bf16[6144,128]{1,0:T(8,128)(2,1)}, bf16[6144,128]{1,0:T(8,128)(2,1)}) custom-call(bf16[6144,384]{1,0:T(8,128)(2,1)} %get-tuple-element.19.q_ref, bf16[384,6144]{1,0:T(8,128)(2,1)} %get-tuple-element.23.qt_ref, bf16[6144,384]{1,0:T(8,128)(2,1)} %get-tuple-element.24.do_ref, ...), custom_call_target="tpu_custom_call" | custom-call | flops 144955146240 | bytes 47185920 | tf_op jit(solution)/shard_map/attn_bwd/pallas_call | solution.py:215
  618.9 3.0 constant_dynamic-update-slice_fusion.2
  622.6 3.2 copy-done.1
  625.8 30.7 %convolution_convert_fusion = bf16[640,3072]{1,0:T(8,128)(2,1)} fusion(bf16[6144,640]{1,0:T(8,128)(2,1)S(1)} %constant_dynamic-update-slice_fusion, bf16[6144,3072]{1,0:T(8,128)(2,1)} %all-gather.7.cloned.1.call-done.h_ref), kind=kOutput, calls=%fused_computation.26 | convolution fusion | flops 24161157120 | bytes 49545216 | tf_op jit(solution)/shard_map/te,td->ed/dot_general | solution.py:271
  656.5 99.8 %all_to_all.10 = bf16[8,768,384]{2,1,0:T(8,128)(2,1)} all-to-all(bf16[8,768,384]{2,1,0:T(8,128)(2,1)} %bitcast.58), channel_id=1, replica_groups=mesh['dp'=1,'sp'=8] {'sp'}, dimensions={0} | all-to-all | bytes 9437184 | tf_op jit(solution)/shard_map/all_to_all | solution.py:263
  756.3 3.9 all-to-all-start.1
  760.1 20.1 %bitcast_convert_fusion = bf16[768,3072]{1,0:T(8,128)(2,1)} fusion(bf16[8,768,384]{2,1,0:T(8,128)(2,1)} %all_to_all.10, bf16[8,384,3072]{2,1,0:T(8,128)(2,1)} %bitcast.59), kind=kOutput, calls=%fused_computation.18 | convolution fusion | flops 14497873920 | bytes 28311552 | tf_op jit(solution)/shard_map/stn,snd->td/dot_general | solution.py:264
  780.3 149.3 %all-to-all-done.1 = bf16[8,768,640]{2,1,0:T(8,128)(2,1)} async-done(((bf16[8,768,640]{2,1,0:T(8,128)(2,1)}), bf16[8,768,640]{2,1,0:T(8,128)(2,1)}, u32[]{:S(2)}, u32[]{:S(2)}) %all-to-all-start.1) | async-done | bytes 7864352 | tf_op jit(solution)/shard_map/all_to_all | solution.py:270
  929.6 9.8 fusion.13
  939.4 9.9 fusion.16
  949.3 26.1 %fusion.10 = (f32[3072]{0:T(1024)S(1)}, f32[768]{0:T(1024)S(1)}, f32[768,3072]{1,0:T(8,128)}) fusion(bf16[768,3072]{1,0:T(8,128)(2,1)} %param.8, f32[768]{0:T(1024)S(1)} %copy-done.11, f32[768]{0:T(1024)S(1)} %copy-done.7, f32[3072]{0:T(1024)S(1)} %copy-done.5, f32[768,3072,1]{1,0,2:T(8,128)} %fusion.13, f32[768,3072,1]{1,0,2:T(8,128)} %fusion.16, ...), kind=kOutput, calls=%fused_computation.13 | convolution fusion | flops 14519103488 | bytes 56656896 | tf_op jit(solution)/shard_map/ste,dse->td/dot_general | solution.py:276
  975.3 22.6 %psum.7 = bf16[3072]{0:T(1024)(128)(2,1)} all-reduce(f32[3072]{0:T(1024)S(1)} %get-tuple-element.31), channel_id=1, replica_groups=mesh['dp'=1,'sp'=8] {'sp'}, use_global_device_ids=true, to_apply=%region_5.6 | all-reduce | flops 3072 | bytes 18432 | tf_op jit(solution)/shard_map/psum | solution.py:280
  997.9 6.7 fusion.29
  1004.7 3.8 add_convert_fusion
  1008.4 11.0 fusion.30
  1019.4 16.7 %slice.27 = bf16[8,384,3072]{2,1,0:T(8,128)(2,1)} slice(bf16[8,640,3072]{2,1,0:T(8,128)(2,1)} %bitcast.51), slice={[0:8], [0:384], [0:3072]} | slice | bytes 37748736 | tf_op jit(solution)/shard_map/slice | solution.py:273
  1036.1 24.6 %copy.27 = bf16[3072,3072]{0,1:T(8,128)(2,1)} copy(bf16[3072,3072]{1,0:T(8,128)(2,1)} %bitcast.49) | data formatting | bytes 37748736 | tf_op jit(solution)/shard_map/reshape | solution.py:273
  1060.7 8.6 copy.29
  1069.3 8.6 copy.28
  1077.9 16.6 %copy.52 = bf16[3072,3072]{1,0:T(8,128)(2,1)} copy(bf16[3072,3072]{1,0:T(8,128)(2,1)} %all-gather.11.cloned.1.call-done) | data formatting | bytes 37748736
  (51 shorter events, 8.9 us)
Async XLA Ops:
  7.2 5.8 copy-start.12
  7.2 188.6 %all-gather.7.cloned.1.call-start = ((), (), s32[]{:S(2)}) async-start(), calls=%async_computation.2 | async-start | bytes 42467328 | tf_op jit(solution)/shard_map/all_gather | solution.py:255
  7.2 3.8 copy-start
  11.0 2.0 copy-start.6
  12.3 0.6 copy-start.8
  12.9 0.6 copy-start.10
  13.5 0.6 copy-start.4
  14.1 5.5 copy-start.13
  18.8 352.9 %all-gather.9.cloned.1.call-start = ((), (), s32[]{:S(2)}) async-start(), calls=%async_computation.3 | async-start | bytes 42467328 | tf_op jit(solution)/shard_map/all_gather | solution.py:256
  19.5 988.9 %all-gather.11.cloned.1.call-start = ((), (), s32[]{:S(2)}) async-start(), calls=%async_computation.4 | async-start | bytes 21233664 | tf_op jit(solution)/shard_map/all_gather | solution.py:267
  393.8 614.6 %all-gather.13.cloned.1.call-start = ((), (), s32[]{:S(2)}) async-start(), calls=%async_computation.5 | async-start | bytes 35389440 | tf_op jit(solution)/shard_map/all_gather | solution.py:272
  618.8 3.0 copy-start.3
  618.9 3.4 copy-start.2
  622.6 3.2 copy-start.1
  756.3 173.3 %all-to-all-start.1 = ((bf16[8,768,640]{2,1,0:T(8,128)(2,1)}), bf16[8,768,640]{2,1,0:T(8,128)(2,1)}, u32[]{:S(2)}, u32[]{:S(2)}) async-start(bf16[8,768,640]{2,1,0:T(8,128)(2,1)} %bitcast.54), calls=%async_computation.1 | async-start | bytes 15728640 | tf_op jit(solution)/shard_map/all_to_all | solution.py:270
  939.4 9.9 copy-start.5
  939.4 9.9 copy-start.7
  939.4 9.9 copy-start.11
  949.3 48.7 %copy-start.9 = (f32[768]{0:T(1024)S(1)}, f32[768]{0:T(1024)}, u32[]{:S(2)}) copy-start(f32[768]{0:T(1024)} %copy-done.8) | copy-start | bytes 9220
Sparse Core Ops, SparseCore 0:
  18.9 176.8 all-gather.6
  197.6 173.9 all-gather.8
  394.0 92.9 all-gather.10
  656.6 271.3 all-gather.12

commit v2 on v1

--- a/solution.py
+++ b/solution.py
@@ -135,14 +135,75 @@
         name="attn_fwd")(q, k, vt)
 
 
-def bwd_kernel(q_ref, qt_ref, do_ref, dot_ref, o_ref, lse_ref, k_ref, v_ref, cos_ref, sin_ref,
-               dq_ref, dk_ref, dv_ref, dlt, dqa, dka, dva, *, bq, bk, t, nh):
+def peer_of(me, rel):
+    bits = [me % 2, (me // 2) % 2, me // 4]
+    flip = [rel % 2, (rel // 2) % 2, rel // 4]
+    out = 0
+    for n in range(3):
+        bit = 1 - bits[n] if flip[n] else bits[n]
+        out = out + bit * (1 << n)
+    return out
+
+
+def remote(src, dst, sems, slot, target):
+    return pltpu.make_async_remote_copy(
+        src_ref=src, dst_ref=dst, send_sem=sems[0].at[slot], recv_sem=sems[1].at[slot],
+        device_id={'sp': target}, device_id_type=pl.DeviceIdType.MESH)
+
+
+def meet_peers(me, n_dev):
+    barrier = pltpu.get_barrier_semaphore()
+    for rel in range(1, n_dev):
+        pl.semaphore_signal(barrier, inc=1, device_id={'sp': peer_of(me, rel)}, device_id_type=pl.DeviceIdType.MESH)
+    pl.semaphore_wait(barrier, n_dev - 1)
+
+
+def bwd_kernel(q_ref, qt_ref, do_ref, dot_ref, o_ref, lse_ref, k_ref, v_ref, cos_ref, sin_ref, o_all,
+               g_own, o_tok, g_tok, dlt, dqa, dka, dva, gqs, gks, gvs, loc_sem, o_send, o_recv, g_send, g_recv,
+               *, bq, bk, t, nh, n_dev):
     h = pl.program_id(0)
     j = pl.program_id(1)
+    nj = t // bk
     nq = t // bq
     rep = bk // D
+    rows = t // n_dev
+    early = nh - 1
     koff = pl.multiple_of(j * bk, bk)
     kc = pl.ds(koff, bk)
+    me = lax.axis_index('sp')
+
+    def rows_of(dev):
+        return pl.ds(pl.multiple_of(dev * rows, rows), rows)
+
+    def o_copy(rel):
+        peer = peer_of(me, rel)
+        return remote(o_all.at[rows_of(peer)], o_tok.at[me], (o_send, o_recv), rel - 1, peer)
+
+    def g_copy(head, rel):
+        peer = peer_of(me, rel)
+        return remote(gqs.at[head, rows_of(peer)], g_tok.at[me, :, pl.ds(head * D, D)],
+                      (g_send.at[head], g_recv.at[head]), rel - 1, peer)
+
+    def o_local():
+        return pltpu.make_async_copy(o_all.at[rows_of(me)], o_tok.at[me], loc_sem.at[0])
+
+    def gq_local(head):
+        return pltpu.make_async_copy(gqs.at[head], g_own.at[:, pl.ds(head * D, D)], loc_sem.at[1 + head])
+
+    def gk_local(jj):
+        r = pl.ds(jj * bk, bk)
+        return pltpu.make_async_copy(gks.at[r], g_own.at[r, pl.ds(nh * D, D)], loc_sem.at[1 + nh + jj])
+
+    def gv_local(jj):
+        r = pl.ds(jj * bk, bk)
+        return pltpu.make_async_copy(gvs.at[r], g_own.at[r, pl.ds((nh + 1) * D, D)], loc_sem.at[1 + nh + nj + jj])
+
+    @pl.when((h == 0) & (j == 0))
+    def _():
+        meet_peers(me, n_dev)
+        for rel in range(1, n_dev):
+            o_copy(rel).start()
+        o_local().start()
 
     @pl.when(j == 0)
     def _():
@@ -188,40 +249,330 @@
 
     lax.fori_loop(first + ratio, nq, body, 0)
 
-    @pl.when(j == pl.num_programs(1) - 1)
-    def _():
-        def fin(i, carry):
-            r = pl.ds(pl.multiple_of(i * bq, bq), bq)
-            dq = dqa[r, :].astype(bf16).astype(f32)
-            dq_ref[r, :] = rotate(dq, cos_ref[r, :], -sin_ref[r, :]).astype(bf16)
-            return carry
-        lax.fori_loop(0, nq, fin, 0)
-
-    @pl.when(h == nh - 1)
-    def _():
-        dk = dka[:, kc].T.astype(bf16).astype(f32)
-        dk_ref[...] = rotate(dk, cos_ref[kc, :], -sin_ref[kc, :]).astype(bf16)
-        dv_ref[...] = dva[:, kc].T.astype(bf16)
-
-
-def attn_bwd(q, qt, do, dot, o, lse, k, v, cos, sin, bq=512, bk=1024):
+    for head in range(nh):
+        @pl.when((j == nj - 1) & (h == head))
+        def _():
+            def fin(i, carry):
+                r = pl.ds(pl.multiple_of(i * bq, bq), bq)
+                dq = dqa[r, :].astype(bf16).astype(f32)
+                gqs[head, r, :] = rotate(dq, cos_ref[r, :], -sin_ref[r, :]).astype(bf16)
+                return carry
+            lax.fori_loop(0, nq, fin, 0)
+            gq_local(head).start()
+            if head < early:
+                for rel in range(1, n_dev):
+                    g_copy(head, rel).start()
+
+    for jj in range(nj):
+        @pl.when((h == nh - 1) & (j == jj))
+        def _():
+            dk = dka[:, jj * bk:(jj + 1) * bk].T.astype(bf16).astype(f32)
+            r = slice(jj * bk, (jj + 1) * bk)
+            gks[r, :] = rotate(dk, cos_ref[r, :], -sin_ref[r, :]).astype(bf16)
+            gvs[r, :] = dva[:, jj * bk:(jj + 1) * bk].T.astype(bf16)
+            gk_local(jj).start()
+            gv_local(jj).start()
+
+    @pl.when((h == nh - 1) & (j == nj - 1))
+    def _():
+        o_local().wait()
+        for head in range(nh):
+            gq_local(head).wait()
+        for jj in range(nj):
+            gk_local(jj).wait()
+            gv_local(jj).wait()
+        for rel in range(1, n_dev):
+            o_copy(rel).wait()
+            for head in range(early):
+                g_copy(head, rel).wait()
+
+
+def attn_bwd(q, qt, do, dot, o, lse, k, v, cos, sin, n_dev, bq=512, bk=1024):
     t, e = q.shape
     nh = e // D
+    nj = t // bk
+    rows = t // n_dev
     col = pl.BlockSpec((t, D), lambda h, j: (0, h))
     row_t = pl.BlockSpec((D, t), lambda h, j: (h, 0))
     kv_in = pl.BlockSpec((bk, D), lambda h, j: (j, 0))
-    kv_out = pl.BlockSpec((bk, D), lambda h, j: (jnp.where(h == nh - 1, j, 0), 0))
     table = pl.BlockSpec((t, D), lambda h, j: (0, 0), pipeline_mode=pl.Buffered(1))
+    hbm = pl.BlockSpec(memory_space=pltpu.HBM)
+    dma = pltpu.SemaphoreType.DMA
     return pl.pallas_call(
-        functools.partial(bwd_kernel, bq=bq, bk=bk, t=t, nh=nh),
-        grid=(nh, t // bk),
-        in_specs=[col, row_t, col, row_t, col, col, kv_in, kv_in, table, table],
-        out_specs=[col, kv_out, kv_out],
-        out_shape=[jax.ShapeDtypeStruct((t, e), bf16), jax.ShapeDtypeStruct((t, D), bf16), jax.ShapeDtypeStruct((t, D), bf16)],
-        scratch_shapes=[pltpu.VMEM((t, D), f32), pltpu.VMEM((t, D), f32), pltpu.VMEM((D, t), f32), pltpu.VMEM((D, t), f32)],
-        compiler_params=pltpu.CompilerParams(vmem_limit_bytes=VMEM_LIMIT, dimension_semantics=("arbitrary", "arbitrary")),
+        functools.partial(bwd_kernel, bq=bq, bk=bk, t=t, nh=nh, n_dev=n_dev),
+        grid=(nh, nj),
+        in_specs=[col, row_t, col, row_t, col, col, kv_in, kv_in, table, table, hbm],
+        out_specs=[hbm, hbm, hbm],
+        out_shape=[jax.ShapeDtypeStruct((t, e + 2 * D), bf16), jax.ShapeDtypeStruct((n_dev, rows, e), bf16),
+                   jax.ShapeDtypeStruct((n_dev, rows, (nh - 1) * D), bf16)],
+        scratch_shapes=[pltpu.VMEM((t, D), f32), pltpu.VMEM((t, D), f32), pltpu.VMEM((D, t), f32), pltpu.VMEM((D, t), f32),
+                        pltpu.VMEM((nh, t, D), bf16), pltpu.VMEM((t, D), bf16), pltpu.VMEM((t, D), bf16),
+                        dma((1 + nh + 2 * nj,)), dma((n_dev - 1,)), dma((n_dev - 1,)), dma((nh - 1, n_dev - 1)), dma((nh - 1, n_dev - 1))],
+        compiler_params=pltpu.CompilerParams(vmem_limit_bytes=VMEM_LIMIT, dimension_semantics=("arbitrary", "arbitrary"),
+                                             collective_id=0, has_side_effects=True),
         cost_estimate=pl.CostEstimate(flops=10 * t * t * e, bytes_accessed=20 * t * e, transcendentals=0),
-        name="attn_bwd")(q, qt, do, dot, o, lse, k, v, cos, sin)
+        name="attn_bwd")(q, qt, do, dot, o, lse, k, v, cos, sin, o)
+
+
+N_CHUNK = 6
+K_STEP = 4
+N_COL = 12
+N_ROW = 6
+
+
+def tail_kernel(h_ref, g_vm, wo_ref, wq_ref, wk_ref, wv_ref, x_ref, lnw_ref, g_own, g_tok, o_tok,
+                a_ref, dx_ref, dl_ref, dw_all, g_late,
+                gt, acc, stage, lhs, dh, dlw, a2a_send, a2a_recv, ag_send, ag_recv, dl_send, dl_recv, st_sem, lhs_sem,
+                *, n_dev):
+    step = pl.program_id(0)
+    me = lax.axis_index('sp')
+    t, width = g_vm.shape
+    rows = t // n_dev
+    qe = width - 2 * D
+    early = g_tok.shape[2]
+    late = width - early
+    dim = x_ref.shape[1]
+    chunk = dim // N_CHUNK
+    kk = t // K_STEP
+    s_a = N_CHUNK * K_STEP
+    s_dh = s_a + N_COL
+    s_ln = s_dh + N_COL
+    cw = dim // N_COL
+    last = s_ln + N_ROW - 1
+    peers = [me] + [peer_of(me, rel) for rel in range(1, n_dev)]
+    SIB, XN, YN, DIAG = 1, 2, 4, 6
+
+    def rows_of(dev):
+        return pl.ds(pl.multiple_of(dev * rows, rows), rows)
+
+    def late_copy(rel):
+        return remote(g_own.at[rows_of(peers[rel]), pl.ds(early, late)], g_late.at[me], (a2a_send, a2a_recv), rel - 1, peers[rel])
+
+    def piece(owner, n):
+        return dw_all.at[pl.ds(pl.multiple_of(owner * dim + n * chunk, chunk), chunk)]
+
+    def ag_copy(kind, n):
+        owner, target = [(0, XN), (0, YN), (0, SIB), ((XN, YN) if n % 2 == 0 else (YN, XN)),
+                         (XN, SIB), (YN, SIB), (DIAG, SIB)][kind]
+        return remote(piece(peers[owner], n), piece(peers[owner], n), (ag_send.at[kind], ag_recv.at[kind]), n, peers[target])
+
+    def dl_copy(rel):
+        return remote(dlw.at[me], dlw.at[me], (dl_send, dl_recv), rel - 1, peers[rel])
+
+    def store_chunk(n):
+        return pltpu.make_async_copy(stage.at[n % 2], piece(me, n), st_sem.at[n % 2])
+
+    def o_load(rel):
+        src = peers[rel]
+        return pltpu.make_async_copy(o_tok.at[src], lhs.at[:, pl.ds(pl.multiple_of(src * qe, D), qe)], lhs_sem.at[0, rel])
+
+    def g_load(rel):
+        src = peers[rel]
+        if rel == 0:
+            first, second, base = g_own.at[rows_of(me), pl.ds(0, early)], g_own.at[rows_of(me)], early
+        else:
+            first, second, base = g_tok.at[src], g_late.at[src], 0
+        n_q = qe - early
+        col = pl.multiple_of(src * qe, D)
+        kcol = pl.multiple_of(dim + src * D, D)
+        vcol = pl.multiple_of(dim + n_dev * D + src * D, D)
+        return [pltpu.make_async_copy(first, lhs.at[:, pl.ds(col, early)], lhs_sem.at[1, rel]),
+                pltpu.make_async_copy(second.at[:, pl.ds(base, n_q)], lhs.at[:, pl.ds(col + early, n_q)], lhs_sem.at[2, rel]),
+                pltpu.make_async_copy(second.at[:, pl.ds(base + n_q, D)], lhs.at[:, pl.ds(kcol, D)], lhs_sem.at[3, rel]),
+                pltpu.make_async_copy(second.at[:, pl.ds(base + n_q + D, D)], lhs.at[:, pl.ds(vcol, D)], lhs_sem.at[4, rel])]
+
+    @pl.when(step == 0)
+    def _():
+        meet_peers(me, n_dev)
+        for rel in (6, 7, 2, 4, 3, 5, 1):
+            late_copy(rel).start()
+        for rel in range(n_dev):
+            o_load(rel).start()
+
+        def flip(i, carry):
+            r = pl.ds(pl.multiple_of(i * 512, 512), 512)
+            gt[:, r] = g_vm[r, :].T
+            return carry
+        lax.fori_loop(0, t // 512, flip, 0)
+
+    for n in range(N_CHUNK):
+        @pl.when(step == (n + 1) * K_STEP)
+        def _():
+            store_chunk(n).wait()
+            for kind in range(3):
+                ag_copy(kind, n).start()
+
+    @pl.when(step < s_a)
+    def _():
+        k = step % K_STEP
+        part = jnp.dot(gt[:, pl.ds(pl.multiple_of(k * kk, kk), kk)], h_ref[...], preferred_element_type=f32)
+
+        @pl.when(k == 0)
+        def _():
+            acc[...] = part
+
+        @pl.when(k > 0)
+        def _():
+            acc[...] += part
+
+    for n in range(N_CHUNK):
+        @pl.when(step == (n + 1) * K_STEP - 1)
+        def _():
+            stage[n % 2] = acc[...].T.astype(bf16)
+            store_chunk(n).start()
+
+    @pl.when(step == s_a)
+    def _():
+        for rel in range(n_dev):
+            o_load(rel).wait()
+
+    @pl.when((step >= s_a) & (step < s_dh))
+    def _():
+        a_ref[...] = jnp.dot(lhs[:, :dim], wo_ref[...], preferred_element_type=f32).astype(bf16)
+
+    @pl.when(step == s_dh)
+    def _():
+        for rel in range(1, n_dev):
+            late_copy(rel).wait_recv()
+        for rel in range(n_dev):
+            for copy in g_load(rel):
+                copy.start()
+        for rel in range(n_dev):
+            for copy in g_load(rel):
+                copy.wait()
+
+    for n in range(N_COL):
+        @pl.when(step == s_dh + n)
+        def _():
+            kv = n_dev * D
+            dh[:, n * cw:(n + 1) * cw] = (
+                lax.dot_general(lhs[:, :dim], wq_ref[...], NT, preferred_element_type=f32)
+                + lax.dot_general(lhs[:, dim:dim + kv], wk_ref[...], NT, preferred_element_type=f32)
+                + lax.dot_general(lhs[:, dim + kv:], wv_ref[...], NT, preferred_element_type=f32))
+
+    @pl.when(step >= s_ln)
+    def _():
+        n = step - s_ln
+        br = rows // N_ROW
+        x = x_ref[...].astype(f32)
+        grad = dh[pl.ds(pl.multiple_of(n * br, br), br), :]
+        cen = x - jnp.mean(x, axis=1, keepdims=True)
+        rstd = lax.rsqrt(jnp.mean(cen * cen, axis=1, keepdims=True) + LN_EPS)
+        xhat = cen * rstd
+        dy = grad * lnw_ref[...].astype(f32)
+        m1 = jnp.mean(dy, axis=1, keepdims=True)
+        m2 = jnp.mean(dy * xhat, axis=1, keepdims=True)
+        dx_ref[...] = (rstd * (dy - m1 - xhat * m2)).astype(bf16)
+        part = jnp.sum((grad * xhat).reshape(br // 8, 8, dim), axis=0)
+
+        @pl.when(n == 0)
+        def _():
+            dlw[me] = part
+
+        @pl.when(n > 0)
+        def _():
+            dlw[me] += part
+
+    @pl.when(step == last)
+    def _():
+        for rel in range(1, n_dev):
+            dl_copy(rel).start()
+        for n in range(N_CHUNK):
+            ag_copy(0, n).wait_recv()
+            if n % 2 == 0:
+                ag_copy(3, n).start()
+            ag_copy(4, n).start()
+            ag_copy(1, n).wait_recv()
+            if n % 2 == 1:
+                ag_copy(3, n).start()
+            ag_copy(5, n).start()
+        for n in range(N_CHUNK):
+            ag_copy(3, n).wait_recv()
+            ag_copy(6, n).start()
+        for rel in range(1, n_dev):
+            dl_copy(rel).wait()
+            late_copy(rel).wait_send()
+        total = dlw[0]
+        for dev in range(1, n_dev):
+            total = total + dlw[dev]
+        dl_ref[...] = jnp.sum(total, axis=0, keepdims=True).astype(bf16)
+        for n in range(N_CHUNK):
+            for kind in (2, 4, 5, 6):
+                ag_copy(kind, n).wait_recv()
+        for n in range(N_CHUNK):
+            for kind in range(7):
+                ag_copy(kind, n).wait_send()
+
+
+def tail(h_all, g_own, g_tok, o_tok, w_o, w_q, w_k, w_v, x, lnw, n_dev):
+    t, dim = h_all.shape
+    width = g_own.shape[1]
+    rows = t // n_dev
+    s_a = N_CHUNK * K_STEP
+    s_dh = s_a + N_COL
+    s_ln = s_dh + N_COL
+    chunk, cw, br = dim // N_CHUNK, dim // N_COL, rows // N_ROW
+    early = g_tok.shape[2]
+    kv = w_k.shape[1]
+    hbm = pl.BlockSpec(memory_space=pltpu.HBM)
+    dma = pltpu.SemaphoreType.DMA
+
+    def h_map(s):
+        c = jnp.minimum(s, s_a - 1)
+        return c % K_STEP, c // K_STEP
+
+    def at(first, count):
+        return lambda s: jnp.clip(s - first, 0, count - 1)
+
+    col_a, col_h, row_l = at(s_a, N_COL), at(s_dh, N_COL), at(s_ln, N_ROW)
+    return pl.pallas_call(
+        functools.partial(tail_kernel, n_dev=n_dev),
+        grid=(s_ln + N_ROW,),
+        in_specs=[pl.BlockSpec((t // K_STEP, chunk), h_map),
+                  pl.BlockSpec((t, width), lambda s: (0, 0), pipeline_mode=pl.Buffered(1)),
+                  pl.BlockSpec((dim, cw), lambda s: (0, col_a(s))),
+                  pl.BlockSpec((cw, dim), lambda s: (col_h(s), 0)),
+                  pl.BlockSpec((cw, kv), lambda s: (col_h(s), 0)),
+                  pl.BlockSpec((cw, kv), lambda s: (col_h(s), 0)),
+                  pl.BlockSpec((br, dim), lambda s: (row_l(s), 0)),
+                  pl.BlockSpec((1, dim), lambda s: (0, 0)),
+                  hbm, hbm, hbm],
+        out_specs=[pl.BlockSpec((rows, cw), lambda s: (0, col_a(s))),
+                   pl.BlockSpec((br, dim), lambda s: (row_l(s), 0)),
+                   pl.BlockSpec((1, dim), lambda s: (0, 0)),
+                   hbm, hbm],
+        out_shape=[jax.ShapeDtypeStruct((rows, dim), bf16), jax.ShapeDtypeStruct((rows, dim), bf16),
+                   jax.ShapeDtypeStruct((1, dim), bf16), jax.ShapeDtypeStruct((n_dev * dim, width), bf16),
+                   jax.ShapeDtypeStruct((n_dev, rows, width - early), bf16)],
+        scratch_shapes=[pltpu.VMEM((width, t), bf16), pltpu.VMEM((width, chunk), f32), pltpu.VMEM((2, chunk, width), bf16),
+                        pltpu.VMEM((rows, dim + 2 * kv), bf16), pltpu.VMEM((rows, dim), f32), pltpu.VMEM((n_dev, 8, dim), f32),
+                        dma((n_dev - 1,)), dma((n_dev - 1,)), dma((7, N_CHUNK)), dma((7, N_CHUNK)),
+                        dma((n_dev - 1,)), dma((n_dev - 1,)), dma((2,)), dma((5, n_dev))],
+        compiler_params=pltpu.CompilerParams(vmem_limit_bytes=VMEM_LIMIT, dimension_semantics=("arbitrary",),
+                                             collective_id=1, has_side_effects=True),
+        name="tail")(h_all, g_own, w_o, w_q, w_k, w_v, x, lnw, g_own, g_tok, o_tok)
+
+
+def spread_kernel(src_ref, q_ref, k_ref, v_ref):
+    n_dev, _, width = src_ref.shape
+    qe = width - 2 * D
+    for dev in range(n_dev):
+        q_ref[:, dev * qe:(dev + 1) * qe] = src_ref[dev, :, :qe]
+        k_ref[:, dev * D:(dev + 1) * D] = src_ref[dev, :, qe:qe + D]
+        v_ref[:, dev * D:(dev + 1) * D] = src_ref[dev, :, qe + D:]
+
+
+def spread(dw_all, bt=256):
+    n_dev, dim, width = dw_all.shape
+    qe = width - 2 * D
+    return pl.pallas_call(
+        spread_kernel,
+        grid=(dim // bt,),
+        in_specs=[pl.BlockSpec((n_dev, bt, width), lambda i: (0, i, 0))],
+        out_specs=[pl.BlockSpec((bt, n_dev * c), lambda i: (i, 0)) for c in (qe, D, D)],
+        out_shape=[jax.ShapeDtypeStruct((dim, n_dev * c), bf16) for c in (qe, D, D)],
+        compiler_params=pltpu.CompilerParams(vmem_limit_bytes=VMEM_LIMIT, dimension_semantics=("arbitrary",)),
+        name="spread")(dw_all)
 
 
 def norm_f32(hid_f32, weight_f32):
@@ -251,8 +602,8 @@
         idx = lax.axis_index('sp')
         qe = w_q.shape[1] // n_dev
         ke = w_k.shape[1] // n_dev
-        normed32, norm_vjp = jax.vjp(norm_f32, hidden.astype(f32), ln_weight.astype(f32))
-        h_all = lax.all_gather(normed32.astype(bf16), 'sp', axis=0, tiled=True)
+        normed = norm_f32(hidden.astype(f32), ln_weight.astype(f32)).astype(bf16)
+        h_all = lax.all_gather(normed, 'sp', axis=0, tiled=True)
         g_all = lax.all_gather(d_attn, 'sp', axis=0, tiled=True)
         cos, sin = rope_tables(lax.all_gather(positions, 'sp', axis=0, tiled=True))
         w_own = jnp.concatenate([lax.dynamic_slice_in_dim(w_q, idx * qe, qe, 1), lax.dynamic_slice_in_dim(w_k, idx * ke, ke, 1),
@@ -260,24 +611,14 @@
         wo_own = lax.dynamic_slice_in_dim(w_o, idx * qe, qe, 0)
         q, qt, k, v, vt = project(h_all, w_own, cos, sin, qe // D)
         o, lse = attn_fwd(q, k, vt)
-        o_tok = lax.all_to_all(o.reshape(n_dev, rows, qe), 'sp', 0, 0)
-        attn_out = jnp.einsum('stn,snd->td', o_tok, w_o.reshape(n_dev, qe, dim), preferred_element_type=f32).astype(bf16)
         do, dot = dout_proj(g_all, wo_own)
         dwo_own = jnp.einsum('te,td->ed', o, g_all, preferred_element_type=f32).astype(bf16)
         dw_o = lax.all_gather(dwo_own, 'sp', axis=0, tiled=True)
-        gq, gk, gv = attn_bwd(q, qt, do, dot, o, lse, k, v, cos, sin)
-        g_own = jnp.concatenate([gq, gk, gv], axis=1)
-        g_tok = lax.all_to_all(g_own.reshape(n_dev, rows, qe + 2 * ke), 'sp', 0, 0)
-        dw_own = jnp.einsum('te,td->ed', g_own, h_all, preferred_element_type=f32).astype(bf16)
-        dw_all = lax.all_gather(dw_own, 'sp', axis=0, tiled=False)
-        dw_q = dw_all[:, :qe].reshape(n_dev * qe, dim).T
-        dw_k = dw_all[:, qe:qe + ke].reshape(n_dev * ke, dim).T
-        dw_v = dw_all[:, qe + ke:].reshape(n_dev * ke, dim).T
-        d_normed = (jnp.einsum('ste,dse->td', g_tok[:, :, :qe], w_q.reshape(dim, n_dev, qe), preferred_element_type=f32)
-                    + jnp.einsum('ste,dse->td', g_tok[:, :, qe:qe + ke], w_k.reshape(dim, n_dev, ke), preferred_element_type=f32)
-                    + jnp.einsum('ste,dse->td', g_tok[:, :, qe + ke:], w_v.reshape(dim, n_dev, ke), preferred_element_type=f32))
-        d_hid, d_lnw = norm_vjp(d_normed)
-        return (attn_out, d_hid.astype(bf16), lax.psum(d_lnw, 'sp').astype(bf16), dw_q, dw_k, dw_v, dw_o)
+        g_own, o_tok, g_tok = attn_bwd(q, qt, do, dot, o, lse, k, v, cos, sin, n_dev)
+        attn_out, d_hid, d_lnw, dw_all, _ = tail(h_all, g_own, g_tok, o_tok, w_o, w_q, w_k, w_v, hidden,
+                                                 ln_weight.reshape(1, dim), n_dev)
+        dw_q, dw_k, dw_v = spread(dw_all.reshape(n_dev, dim, qe + 2 * ke))
+        return attn_out, d_hid, d_lnw.reshape(dim), dw_q, dw_k, dw_v, dw_o
 
     return jax.shard_map(local_step, mesh=mesh,
                          in_specs=(row_spec, pos_spec, row_spec, P(None), full_spec, full_spec, full_spec, full_spec),

time: 1110 us -> 876 us (0.79)
  Pallas kernels: 364 us -> 590 us
  waiting for transfers between devices: 327 us -> 177 us
  blocking collectives: 136 us -> 14 us
  matrix products: 119 us -> 22.2 us
  local copies, waits for them, and re-layouts: 102 us -> 27.3 us
    pallas_call x1 -> x3, Pallas kernels: 194 us -> 421 us  [the longest x1 199 us: tail(): pl.pallas_call(functools.partial(tail_kernel, n_dev=n_dev), grid=(s_ln +...]
    all_to_all x1 -> x0, waiting for transfers between devices: 149 us -> none  [local_step(): g_tok = lax.all_to_all(g_own.reshape(n_dev, rows, qe + 2 * ke), 'sp', 0, 0)]
    all_to_all x1 -> x0, blocking collectives: 99.8 us -> none  [local_step(): o_tok = lax.all_to_all(o.reshape(n_dev, rows, qe), 'sp', 0, 0)]
    dot_general x5 -> x0, matrix products: 96.5 us -> none  [the longest x1 30.7 us: local_step(): jnp.einsum('te,td->ed', g_own, h_all, preferred_element_type=f32)]
    reshape x3 -> x1, local copies, waits for them, and re-layouts: 41.8 us -> 0.6 us  [local_step(): ln_weight.reshape(1, dim)]
    slice x2 -> x0, local copies, waits for them, and re-layouts: 27.6 us -> none  [the longest x1 16.7 us: local_step(): dw_q = dw_all[:, :qe].reshape(n_dev * qe, dim).T]
    psum x1 -> x0, blocking collectives: 22.6 us -> none  [local_step(): lax.psum(d_lnw, 'sp').astype(bf16)]
    unnamed x32 -> x14, local copies, waits for them, and re-layouts: 25.5 us -> 20 us
  transfers between devices with their start and end apart: 5 -> 3, of which waited for: 3 -> 2; matrix products, arithmetic and copies ran while one was open for 12% -> 3% of each run, Pallas kernels for 33% -> 68%
where the time goes in v2:
time: 876 us; the launch traced here: 871 us
  Pallas kernels  590 us (67%)
  waiting for transfers between devices  177 us (20%)
  local copies, waits for them, and re-layouts  27.3 us (3%)
  other arithmetic  25.7 us (3%)
  matrix products  22.2 us (3%)
  between operations  14.2 us (2%)
  blocking collectives  14 us (2%)
    pallas_call x1, Pallas kernels, tail(): pl.pallas_call(functools.partial(tail_kernel, n_dev=n_dev), grid=(s_ln +...  199 us
    pallas_call x1, Pallas kernels, attn_bwd(): pl.pallas_call(functools.partial(bwd_kernel, bq=bq, bk=bk, t=t, nh=nh, n_...  197 us
    all_gather x1, waiting for transfers between devices, local_step(): h_all = lax.all_gather(normed, 'sp', axis=0, tiled=True)  143 us
    pallas_call x1, Pallas kernels, attn_fwd(): pl.pallas_call(functools.partial(fwd_kernel, bq=bq, bk=bk, nh=nh), grid=(...  102 us
    pallas_call x1, Pallas kernels, project(): pl.pallas_call(functools.partial(proj_kernel, nh=nh), grid=(t // bt,), in...  39.8 us
    all_gather x1, waiting for transfers between devices, local_step(): g_all = lax.all_gather(d_attn, 'sp', axis=0, tiled=True)  34 us
    pallas_call x1, Pallas kernels, dout_proj(): pl.pallas_call(dout_kernel, grid=(t // bt,), in_specs=[pl.BlockSpec((bt,...  27.4 us
    pallas_call x1, Pallas kernels, spread(): pl.pallas_call(spread_kernel, grid=(dim // bt,), in_specs=[pl.BlockSpec((...  25.2 us
  transfers between devices with their start and end apart: 3, of which 2 were waited for; matrix products, arithmetic and copies ran while one was open for 3% of the time, Pallas kernels for 68%

profile of v2, /device:TPU:0, one launch (start us, length us, event | category | flops | bytes accessed | tf_op | source)
XLA Modules:
  0.0 871.4 jit_solution(14360691831829994802)
XLA Ops:
  7.2 0.0 all-gather.5.cloned.1.call-start
  7.2 0.0 copy-start
  7.2 3.2 convert_reduce_fusion
  10.4 0.6 copy-done
  11.0 1.4 fusion.2
  12.4 4.6 fusion.4
  17.0 0.0 all-gather.5.cloned.1.call-update
  17.0 0.0 all-gather.7.cloned.1.call-start
  17.1 0.7 all-gather.7.cloned.1.call-update
  17.8 0.0 all-gather.9.cloned.1.call-start
  17.9 14.0 %all-gather = s32[8,1,768]{2,1,0:T(1,128)S(1)} all-gather(s32[1,1,768]{2,1,0:T(1,128)S(1)} %reshape.65), channel_id=1, replica_groups=mesh['dp'=1,'sp'=8] {'sp'}, dimensions={0}, use_global_device_ids=true | all-gather | bytes 27648 | tf_op jit(solution)/shard_map/all_gather | solution.py:608
  31.9 1.5 constant_dynamic-slice_fusion.1
  33.4 1.9 constant_dynamic-slice_fusion.3
  35.4 2.1 pad_maximum_fusion.w_ref
  37.5 13.7 %negate_select_fusion = (f32[6144,128]{1,0:T(8,128)}, f32[6144,128]{1,0:T(8,128)}) fusion(f32[128]{0:T(128)S(1)} %fusion.8, f32[6144]{0:T(1024)S(1)} %bitcast.5, pred[128]{0:T(512)(128)(4,1)S(1)} %broadcast_compare_fusion), kind=kLoop, calls=%fused_computation.7 | loop fusion | flops 2359296 | bytes 6316672 | tf_op jit(solution)/shard_map/jit(_where)/select_n | solution.py:590
  51.3 142.8 %all-gather.5.cloned.1.call-done.h_ref = bf16[6144,3072]{1,0:T(8,128)(2,1)} async-done(((bf16[768,3072]{1,0:T(8,128)(2,1)}), bf16[6144,3072]{1,0:T(8,128)(2,1)}) %all-gather.5.cloned.1.call-update) | async-done | bytes 37748752 | tf_op jit(solution)/shard_map/all_gather | solution.py:606
  194.0 39.8 %qkv_proj.1 = (bf16[6144,384]{1,0:T(8,128)(2,1)}, bf16[384,6144]{1,0:T(8,128)(2,1)}, bf16[6144,128]{1,0:T(8,128)(2,1)}, bf16[6144,128]{1,0:T(8,128)(2,1)}, bf16[128,6144]{1,0:T(8,128)(2,1)}) custom-call(bf16[6144,3072]{1,0:T(8,128)(2,1)} %all-gather.5.cloned.1.call-done.h_ref, bf16[3072,640]{1,0:T(8,128)(2,1)} %pad_maximum_fusion.w_ref, ...), custom_call_target="tpu_custom_call" | custom-call | flops 24159191040 | bytes 37748736 | tf_op jit(solution)/shard_map/qkv_proj/pallas_call | solution.py:45
  233.9 102.1 %attn_fwd.1 = (bf16[6144,384]{1,0:T(8,128)(2,1)}, f32[6144,384]{1,0:T(8,128)}) custom-call(bf16[6144,384]{1,0:T(8,128)(2,1)} %get-tuple-element.26.q_ref, bf16[6144,128]{1,0:T(8,128)(2,1)} %get-tuple-element.30.k_ref, bf16[128,6144]{1,0:T(8,128)(2,1)} %get-tuple-element.31.vt_ref), custom_call_target="tpu_custom_call" | custom-call | flops 57982058496 | bytes 18874368 | tf_op jit(solution)/shard_map/attn_fwd/pallas_call | solution.py:126
  335.9 34.0 %all-gather.7.cloned.1.call-done.g_ref = bf16[6144,3072]{1,0:T(8,128)(2,1)} async-done(((bf16[768,3072]{1,0:T(8,128)(2,1)}), bf16[6144,3072]{1,0:T(8,128)(2,1)}) %all-gather.7.cloned.1.call-update) | async-done | bytes 37748752 | tf_op jit(solution)/shard_map/all_gather | solution.py:607
  369.9 22.2 %convolution_convert_fusion = bf16[384,3072]{1,0:T(8,128)(2,1)} fusion(bf16[6144,384]{1,0:T(8,128)(2,1)} %get-tuple-element.32.o_ref.o_all, bf16[6144,3072]{1,0:T(8,128)(2,1)} %all-gather.7.cloned.1.call-done.g_ref), kind=kOutput, calls=%fused_computation.10 | convolution fusion | flops 14496694272 | bytes 44826624 | tf_op jit(solution)/shard_map/te,td->ed/dot_general | solution.py:615
  392.1 0.0 all-gather.9.cloned.1.call-update
  392.1 0.6 reshape.62.lnw_ref
  392.7 3.2 constant_dynamic-slice_fusion.w_ref
  395.9 27.4 %dout_proj.1 = (bf16[6144,384]{1,0:T(8,128)(2,1)}, bf16[384,6144]{1,0:T(8,128)(2,1)}) custom-call(bf16[6144,3072]{1,0:T(8,128)(2,1)} %all-gather.7.cloned.1.call-done.g_ref, bf16[384,3072]{1,0:T(8,128)(2,1)} %constant_dynamic-slice_fusion.w_ref), custom_call_target="tpu_custom_call" | custom-call | flops 14495514624 | bytes 37748736 | tf_op jit(solution)/shard_map/dout_proj/pallas_call | solution.py:66
  423.3 196.8 %attn_bwd.1 = (bf16[6144,640]{1,0:T(8,128)(2,1)}, bf16[8,768,384]{2,1,0:T(8,128)(2,1)}, bf16[8,768,256]{2,1,0:T(8,128)(2,1)}) custom-call(bf16[6144,384]{1,0:T(8,128)(2,1)} %get-tuple-element.26.q_ref, bf16[384,6144]{1,0:T(8,128)(2,1)} %get-tuple-element.27.qt_ref, bf16[6144,384]{1,0:T(8,128)(2,1)} %get-tuple-element.28.do_ref, ...), custom_call_target="tpu_custom_call" | custom-call | flops 144955146240 | bytes 47185920 | tf_op jit(solution)/shard_map/attn_bwd/pallas_call | solution.py:301
  620.2 199.0 %tail.1 = (bf16[768,3072]{1,0:T(8,128)(2,1)}, bf16[768,3072]{1,0:T(8,128)(2,1)}, bf16[1,3072]{1,0:T(2,128)(2,1)}, bf16[24576,640]{1,0:T(8,128)(2,1)}, bf16[8,768,384]{2,1,0:T(8,128)(2,1)}) custom-call(bf16[6144,3072]{1,0:T(8,128)(2,1)} %all-gather.5.cloned.1.call-done.h_ref, bf16[6144,640]{1,0:T(8,128)(2,1)} %get-tuple-element.35.g_vm.g_own, ...), custom_call_target="tpu_custom_call" | custom-call | tf_op jit(solution)/shard_map/tail/pallas_call | solution.py:528
  819.2 25.2 %spread.1 = (bf16[3072,3072]{1,0:T(8,128)(2,1)}, bf16[3072,1024]{1,0:T(8,128)(2,1)}, bf16[3072,1024]{1,0:T(8,128)(2,1)}) custom-call(bf16[8,3072,640]{2,1,0:T(8,128)(2,1)} %bitcast.4), custom_call_target="tpu_custom_call" | custom-call | tf_op jit(solution)/shard_map/spread/pallas_call | solution.py:568
  844.4 0.6 reduce
  845.1 5.2 copy.18
  850.3 5.8 copy.19
  856.1 1.6 copy-done.1
  857.7 6.8 copy.20
  (15 shorter events, 0.1 us)
Async XLA Ops:
  7.2 5.2 copy-start.2
  7.2 186.8 %all-gather.5.cloned.1.call-start = ((), (), s32[]{:S(2)}) async-start(), calls=%async_computation | async-start | bytes 42467328 | tf_op jit(solution)/shard_map/all_gather | solution.py:606
  7.2 3.8 copy-start
  17.0 0.8 copy-start.4
  17.0 352.9 %all-gather.7.cloned.1.call-start = ((), (), s32[]{:S(2)}) async-start(), calls=%async_computation.1 | async-start | bytes 42467328 | tf_op jit(solution)/shard_map/all_gather | solution.py:607
  17.8 827.3 %all-gather.9.cloned.1.call-start = ((), (), s32[]{:S(2)}) async-start(), calls=%async_computation.2 | async-start | bytes 21233664 | tf_op jit(solution)/shard_map/all_gather | solution.py:616
  819.2 25.2 %copy-start.3 = (bf16[1,3072]{1,0:T(2,128)(2,1)S(1)}, bf16[1,3072]{1,0:T(2,128)(2,1)}, u32[]{:S(2)}) copy-start(bf16[1,3072]{1,0:T(2,128)(2,1)} %get-tuple-element.40) | copy-start | bytes 18436
  845.1 12.6 %copy-start.1 = (bf16[3072,3072]{1,0:T(8,128)(2,1)S(1)}, bf16[3072,3072]{1,0:T(8,128)(2,1)}, u32[]{:S(2)}) copy-start(bf16[3072,3072]{1,0:T(8,128)(2,1)} %all-gather.9.cloned.1.call-done) | copy-start | bytes 56623108
Sparse Core Ops, SparseCore 0:
  17.1 176.8 all-gather.4
  195.8 173.9 all-gather.6
  392.2 151.9 all-gather.8

commit v3 on v2

v3 whole, which is shorter than its diff:
```python
import functools
import math
import jax
import jax.numpy as jnp
from jax import lax
from jax.experimental import pallas as pl
from jax.experimental.pallas import tpu as pltpu
from jax.sharding import PartitionSpec as P

D = 128
LN_EPS = 1e-5
ROPE_BASE = 10000.0
SCALE = D ** -0.5
SCALE2 = SCALE * math.log2(math.e)
NT = (((1,), (1,)), ((), ()))
f32 = jnp.float32
bf16 = jnp.bfloat16
VMEM_LIMIT = 60 * 2 ** 20
shape = jax.ShapeDtypeStruct
dma = pltpu.SemaphoreType.DMA
hbm = pl.BlockSpec(memory_space=pltpu.HBM)


def params(axes=1, **more):
    more.update(has_side_effects=bool(more))
    return pltpu.CompilerParams(vmem_limit_bytes=VMEM_LIMIT, dimension_semantics=("arbitrary",) * axes, **more)


def fixed(i):
    return 0, 0


def rows_at(i):
    return i, 0


def cols_at(i):
    return 0, i


def others(n_dev):
    return range(1, n_dev)


def lanes(h):
    return slice(h * D, (h + 1) * D)


def norm_f32(hid_f32, weight_f32):
    mean_val = jnp.mean(hid_f32, axis=-1, keepdims=True)
    centered = hid_f32 - mean_val
    var_val = jnp.mean(centered * centered, axis=-1, keepdims=True)
    return centered * lax.rsqrt(var_val + LN_EPS) * weight_f32


SIB, XN, YN, DIAG = 1, 2, 4, 6


def peer_of(me, rel):
    mine = (me % 2, (me // 2) % 2, me // 4)
    flip = (rel % 2, (rel // 2) % 2, rel // 4)
    return sum(((mine[n] + flip[n]) % 2) * (1 << n) for n in range(3))


def remote(src, dst, sems, slot, target):
    return pltpu.make_async_remote_copy(
        src_ref=src, dst_ref=dst, send_sem=sems[0].at[slot], recv_sem=sems[1].at[slot],
        device_id={'sp': target}, device_id_type=pl.DeviceIdType.MESH)


def meet_peers(me, n_dev):
    barrier = pltpu.get_barrier_semaphore()
    for rel in others(n_dev):
        pl.semaphore_signal(barrier, device_id={'sp': peer_of(me, rel)}, device_id_type=pl.DeviceIdType.MESH)
    pl.semaphore_wait(barrier, n_dev - 1)


def gather_copy(kind, n, own, piece, sems, me):
    if kind == 3:
        owner, target = (XN, YN) if n % 2 == 0 else (YN, XN)
    else:
        owner, target = {0: (0, XN), 1: (0, YN), 2: (0, SIB), 4: (XN, SIB), 5: (YN, SIB), 6: (DIAG, SIB)}[kind]
    dst = piece(peer_of(me, owner), n)
    return remote(own(n) if owner == 0 else dst, dst, (sems[0].at[kind], sems[1].at[kind]), n, peer_of(me, target))


def rotate(val, cos, sin):
    even = lax.rem(lax.broadcasted_iota(jnp.int32, val.shape, 1), 2) == 0
    swapped = jnp.where(even, pltpu.roll(val, D - 1, 1), pltpu.roll(val, 1, 1))
    return val * cos + swapped * sin


N_SUB = 3


def item_of(s, n_dev):
    n_mid = 4 * N_SUB
    first = 2 * N_SUB
    u, w = s - first, s - first - n_mid
    r = u % 4
    rel = jnp.where(s < first, s // N_SUB, jnp.where(s < first + n_mid, 2 + 2 * (r % 2) + r // 2, 6 + w % 2))
    m = jnp.where(s < first, s % N_SUB, jnp.where(s < first + n_mid, u // 4, w // 2))
    return rel, m


def items(n_dev):
    out = [(rel, m) for rel in (0, SIB) for m in range(N_SUB)]
    out += [(rel, m) for m in range(N_SUB) for rel in (XN, YN, XN + 1, YN + 1)]
    return out + [(rel, m) for m in range(N_SUB) for rel in (DIAG, DIAG + 1)]


def start_kernel(x_ref, lnw_ref, wq_hbm, wk_hbm, wv_hbm, freq_ref, pos_ref, q_ref, qt_ref, k_ref, v_ref, vt_ref, cos_ref, sin_ref, h_all,
                 w_ref, hs, buf, pos_all, w_sem, loc_sem, ld_sem, pos_send, pos_recv, ag_send, ag_recv, *, n_dev, nh):
    step = pl.program_id(0)
    me = lax.axis_index('sp')
    rows = x_ref.shape[0]
    size = rows // (2 * N_SUB)
    sub = 2 * size
    order = items(n_dev)
    rel_t, m_t = item_of(step, n_dev)
    owner_t = peer_of(me, rel_t)

    def own(n):
        return hs.at[pl.ds(pl.multiple_of(n * size, size), size)]

    def piece(owner, n):
        return h_all.at[pl.ds(pl.multiple_of(owner * rows + n * size, size), size)]

    def copy(kind, n):
        return gather_copy(kind, n, own, piece, (ag_send, ag_recv), me)

    def pos_copy(rel):
        return remote(pos_all.at[me], pos_all.at[me], (pos_send, pos_recv), rel, peer_of(me, rel))

    def keep_own():
        return pltpu.make_async_copy(hs, h_all.at[pl.ds(pl.multiple_of(me * rows, rows), rows)], loc_sem)

    def load(i):
        rel, m = order[i]
        src = h_all.at[pl.ds(pl.multiple_of(peer_of(me, rel) * rows + m * sub, sub), sub)]
        return pltpu.make_async_copy(src, buf.at[i % 2], ld_sem.at[i % 2])

    def arrive(i):
        rel, m = order[i]
        for n in (2 * m, 2 * m + 1):
            if rel == SIB:
                copy(2, n).wait_recv()
            elif rel in (XN, YN):
                copy(0 if rel == XN else 1, n).wait_recv()
                if (rel == XN) == (n % 2 == 0):
                    copy(3, n).start()
                copy(4 if rel == XN else 5, n).start()
            elif rel in (XN + 1, YN + 1):
                copy(4 if rel == XN + 1 else 5, n).wait_recv()
            elif rel == DIAG:
                copy(3, n).wait_recv()
                copy(6, n).start()
            elif rel == DIAG + 1:
                copy(6, n).wait_recv()

    def w_load(i):
        col, size_w, src = ((0, nh * D, wq_hbm), (nh * D, D, wk_hbm), ((nh + 1) * D, D, wv_hbm))[i]
        return pltpu.make_async_copy(src.at[:, pl.ds(pl.multiple_of(me * size_w, D), size_w)], w_ref.at[:, pl.ds(col, size_w)], w_sem.at[i])

    @pl.when(step == 0)
    def _():
        for i in range(3):
            w_load(i).start()
        pos_all[me] = pos_ref[:]
        meet_peers(me, n_dev)

        def norm(n, carry):
            r = pl.ds(pl.multiple_of(n * size, size), size)
            hs[r, :] = norm_f32(x_ref[r, :].astype(f32), lnw_ref[:].astype(f32)).astype(bf16)

            @pl.when(n > 0)
            def _():
                for kind in range(3):
                    copy(kind, n - 1).start()
            return carry
        lax.fori_loop(0, 2 * N_SUB, norm, 0)
        for rel in others(n_dev):
            pos_copy(rel).start()
        for kind in range(3):
            copy(kind, 2 * N_SUB - 1).start()
        keep_own().start()
        keep_own().wait()
        load(0).start()
        for i in range(3):
            w_load(i).wait()

    for i in range(1, len(order)):
        @pl.when(step == i - 1)
        def _():
            if i == N_SUB:
                for rel in others(n_dev):
                    pos_copy(rel).wait_recv()
            arrive(i)
            load(i).start()

    slot = step % 2
    pltpu.make_async_copy(h_all.at[pl.ds(0, sub)], buf.at[slot], ld_sem.at[slot]).wait()
    tile = pos_all[owner_t, m_t].astype(f32)
    pos = jnp.concatenate([jnp.broadcast_to(tile[i:i + 1, :], (D, D)).T for i in range(sub // D)], axis=0)
    angles = pos * freq_ref[:]
    cos = jnp.cos(angles)
    sin = jnp.sin(angles)
    sin = jnp.where(lax.rem(lax.broadcasted_iota(jnp.int32, sin.shape, 1), 2) == 0, -sin, sin)
    cos_ref[:] = cos
    sin_ref[:] = sin
    res = jnp.dot(buf[slot], w_ref[:], preferred_element_type=f32)
    for n in range(nh):
        rot = rotate(res[:, lanes(n)], cos, sin).astype(bf16)
        q_ref[:, lanes(n)] = rot
        qt_ref[lanes(n), :] = rot.T
    k_ref[:] = rotate(res[:, lanes(nh)], cos, sin).astype(bf16)
    v = res[:, (nh + 1) * D:].astype(bf16)
    v_ref[:] = v
    vt_ref[:] = v.T

    @pl.when(step == len(order) - 1)
    def _():
        for rel in others(n_dev):
            pos_copy(rel).wait_send()
        for n in range(2 * N_SUB):
            for kind in range(7):
                copy(kind, n).wait_send()


def start(x, lnw, w_q, w_k, w_v, freq, pos, nh, n_dev):
    rows, dim = x.shape
    t = rows * n_dev
    sub = rows // N_SUB
    whole = lambda a: pl.BlockSpec(a.shape, lambda s: (0,) * a.ndim, pipeline_mode=pl.Buffered(1))

    def at(s):
        rel, m = item_of(s, n_dev)
        return peer_of(lax.axis_index('sp'), rel) * N_SUB + m

    row = lambda c: pl.BlockSpec((sub, c), lambda s: (at(s), 0))
    col = lambda r: pl.BlockSpec((r, sub), lambda s: (0, at(s)))
    return pl.pallas_call(
        functools.partial(start_kernel, n_dev=n_dev, nh=nh),
        grid=(n_dev * N_SUB,),
        in_specs=[whole(x), whole(lnw), hbm, hbm, hbm, whole(freq), whole(pos)],
        out_specs=[row(nh * D), col(nh * D), row(D), row(D), col(D), row(D), row(D), hbm],
        out_shape=[shape((t, nh * D), bf16), shape((nh * D, t), bf16), shape((t, D), bf16), shape((t, D), bf16), shape((D, t), bf16),
                   shape((t, D), f32), shape((t, D), f32), shape((t, dim), bf16)],
        scratch_shapes=[pltpu.VMEM((dim, (nh + 2) * D), bf16), pltpu.VMEM((rows, dim), bf16), pltpu.VMEM((2, sub, dim), bf16),
                        pltpu.VMEM((n_dev,) + pos.shape, jnp.int32), dma((3,)), dma, dma((2,)), dma((n_dev,)), dma((n_dev,)), dma((7, 2 * N_SUB)), dma((7, 2 * N_SUB))],
        compiler_params=params(1, collective_id=4),
        name="start")(x, lnw, w_q, w_k, w_v, freq, pos)


def mid_kernel(g_blk, ot_ref, w_ref, g_own, do_ref, dot_ref, dwo_ref, g_rest, acc, buf, ld_sem, ag_send, ag_recv, *, n_dev, rows, first):
    step = pl.program_id(0)
    me = lax.axis_index('sp')
    rest = rows - first
    half = rest // 2
    order = (0, SIB, XN, YN, XN + 1, YN + 1, DIAG, DIAG + 1)

    def own(n):
        return g_own.at[pl.ds(first + n * half, half)]

    def piece(owner, n):
        return g_rest.at[pl.ds(pl.multiple_of(owner * rest + n * half, half), half)]

    def copy(kind, n):
        return gather_copy(kind, n, own, piece, (ag_send, ag_recv), me)

    def load(i):
        owner = peer_of(me, order[i])
        src = g_own.at[pl.ds(first, rest)] if i == 0 else g_rest.at[pl.ds(pl.multiple_of(owner * rest, rest), rest)]
        return pltpu.make_async_copy(src, buf.at[i % 2], ld_sem.at[i % 2])

    def compute(g, row0, size):
        r = pl.ds(row0, size)
        val = lax.dot_general(g, w_ref[:], NT, preferred_element_type=f32).astype(bf16)
        do_ref[r, :] = val
        dot_ref[:, r] = val.T
        acc[:] += jnp.dot(ot_ref[:, r], g, preferred_element_type=f32)

    @pl.when(step == 0)
    def _():
        meet_peers(me, n_dev)
        for n in range(2):
            for kind in range(3):
                copy(kind, n).start()
        acc[:] = jnp.zeros_like(acc)

    @pl.when(step == 5)
    def _():
        copy(0, 0).wait_recv()
        copy(3, 0).start()
        copy(4, 0).start()

    @pl.when(step == n_dev)
    def _():
        copy(1, 1).wait_recv()
        copy(3, 1).start()
        copy(5, 1).start()
        copy(0, 1).wait_recv()
        copy(4, 1).start()
        copy(1, 0).wait_recv()
        copy(5, 0).start()

    waits = {1: ((2, 0), (2, 1)), 4: ((4, 0), (4, 1)), 5: ((5, 0), (5, 1)), 6: ((3, 0), (3, 1)), 7: ((6, 0), (6, 1))}
    for i in range(n_dev):
        @pl.when(step == n_dev - 1 + i)
        def _():
            for kind, n in waits.get(i, ()):
                copy(kind, n).wait_recv()
                if kind == 3:
                    copy(6, n).start()
            load(i).start()

    @pl.when(step < n_dev)
    def _():
        compute(g_blk[:], pl.multiple_of(step * rows, D), first)

    for i in range(n_dev):
        @pl.when(step == n_dev + i)
        def _():
            load(i).wait()
            compute(buf[i % 2], pl.multiple_of(peer_of(me, order[i]) * rows + first, D), rest)

    @pl.when(step == 2 * n_dev - 1)
    def _():
        dwo_ref[:] = acc[:].astype(bf16)
        for n in range(2):
            for kind in range(7):
                copy(kind, n).wait_send()


def mid(g_first, ot, w, g_own, n_dev):
    dim = g_own.shape[1]
    rows = g_own.shape[0]
    first = g_first.shape[0] // n_dev
    rest = rows - first
    e, t = ot.shape
    whole = lambda a, b: pl.BlockSpec((a, b), fixed, pipeline_mode=pl.Buffered(1))
    const = lambda a, b: pl.BlockSpec((a, b), fixed)
    w_spec = pl.BlockSpec((e, dim), lambda i: (lax.axis_index('sp'), 0), pipeline_mode=pl.Buffered(1))
    return pl.pallas_call(
        functools.partial(mid_kernel, n_dev=n_dev, rows=rows, first=first),
        grid=(2 * n_dev,),
        in_specs=[pl.BlockSpec((first, dim), lambda i: (jnp.minimum(i, n_dev - 1), 0)), whole(e, t), w_spec, hbm],
        out_specs=[const(t, e), const(e, t), const(e, dim), hbm],
        out_shape=[shape((t, e), bf16), shape((e, t), bf16), shape((e, dim), bf16),
                   shape((n_dev * rest, dim), bf16)],
        scratch_shapes=[pltpu.VMEM((e, dim), f32), pltpu.VMEM((2, rest, dim), bf16), dma((2,)), dma((7, 2)), dma((7, 2))],
        compiler_params=params(1, collective_id=3),
        name="mid")(g_first, ot, w, g_own)


def fwd_kernel(q_ref, k_ref, vt_ref, g_own, o_ref, ot_ref, lse_ref, g_first, acc, m_ref, l_ref, loc_sem, ag_send, ag_recv,
               *, bq, bk, nh, n_dev, first, n_piece):
    i = pl.program_id(0)
    nq = pl.num_programs(0)
    me = lax.axis_index('sp')
    size = first // n_piece

    def own(n):
        return g_own.at[pl.ds(n * size, size)]

    def piece(owner, n):
        return g_first.at[pl.ds(pl.multiple_of(owner * first + n * size, size), size)]

    def copy(kind, n):
        return gather_copy(kind, n, own, piece, (ag_send, ag_recv), me)

    def keep_own():
        return pltpu.make_async_copy(g_own.at[pl.ds(0, first)], g_first.at[pl.ds(pl.multiple_of(me * first, first), first)], loc_sem)

    def pass_on(n):
        copy(0, n).wait_recv()
        copy(1, n).wait_recv()
        copy(3, n).start()
        copy(4, n).start()
        copy(5, n).start()

    @pl.when(i == 0)
    def _():
        meet_peers(me, n_dev)
        for n in range(n_piece):
            for kind in range(3):
                copy(kind, n).start()
        keep_own().start()

    @pl.when(i == nq - 2)
    def _():
        for n in range(n_piece // 2):
            pass_on(n)

    @pl.when(i == nq - 1)
    def _():
        for n in range(n_piece // 2, n_piece):
            pass_on(n)

    for h in range(nh):
        m_ref[h:h + 1, :] = jnp.full((1, bq), -1e30, f32)
        l_ref[h:h + 1, :] = jnp.zeros((1, bq), f32)
    acc[:] = jnp.zeros_like(acc)

    def step(off, diag):
        q0 = 0 if diag is None else diag
        kb = k_ref[pl.ds(off, bk), :]
        vt = vt_ref[:, pl.ds(off, bk)]
        if diag is not None:
            ki = lax.broadcasted_iota(jnp.int32, (bk, bq - q0), 0)
            qi = lax.broadcasted_iota(jnp.int32, (bk, bq - q0), 1)
            keep = ki <= qi
        ss = [lax.dot_general(kb, q_ref[q0:, lanes(h)], NT, preferred_element_type=f32) for h in range(nh)]
        for h in range(nh):
            s = ss[h]
            if diag is not None:
                s = jnp.where(keep, s, -1e30)
            m_old = m_ref[h:h + 1, q0:]
            m_new = jnp.maximum(m_old, jnp.max(s, axis=0, keepdims=True))
            p = jnp.exp2(s * SCALE2 - m_new * SCALE2)
            alpha = jnp.exp2((m_old - m_new) * SCALE2)
            m_ref[h:h + 1, q0:] = m_new
            l_ref[h:h + 1, q0:] = l_ref[h:h + 1, q0:] * alpha + jnp.sum(p, axis=0, keepdims=True)
            pv = jnp.dot(vt, p.astype(bf16), preferred_element_type=f32)
            acc[lanes(h), q0:] = acc[lanes(h), q0:] * alpha + pv

    ratio = bq // bk

    def body(j, carry):
        step(pl.multiple_of(j * bk, bk), None)
        return carry

    lax.fori_loop(0, i * ratio, body, 0)
    for d in range(ratio):
        step(pl.multiple_of(i * bq + d * bk, bk), d * bk)
    for h in range(nh):
        m = m_ref[h:h + 1, :]
        l = l_ref[h:h + 1, :]
        out_t = acc[lanes(h), :] * (1.0 / l)
        o_ref[:, lanes(h)] = out_t.T.astype(bf16)
        ot_ref[lanes(h), :] = out_t.astype(bf16)
        lse_ref[:, lanes(h)] = jnp.broadcast_to(m * SCALE2 + jnp.log2(l), (D, bq)).T

    @pl.when(i == nq - 1)
    def _():
        for n in range(n_piece):
            copy(3, n).wait_recv()
            copy(6, n).start()
        keep_own().wait()
        for n in range(n_piece):
            for kind in (2, 4, 5, 6):
                copy(kind, n).wait_recv()
            for kind in range(7):
                copy(kind, n).wait_send()


def attn_fwd(q, k, vt, g_own, first, n_dev, bq=1024, bk=512, n_piece=4):
    t, e = q.shape
    nh = e // D
    row = pl.BlockSpec((bq, e), rows_at)
    return pl.pallas_call(
        functools.partial(fwd_kernel, bq=bq, bk=bk, nh=nh, n_dev=n_dev, first=first, n_piece=n_piece),
        grid=(t // bq,),
        in_specs=[row, pl.BlockSpec((t, D), fixed), pl.BlockSpec((D, t), fixed), hbm],
        out_specs=[row, pl.BlockSpec((e, bq), cols_at), row, hbm],
        out_shape=[shape((t, e), bf16), shape((e, t), bf16), shape((t, e), f32),
                   shape((n_dev * first, g_own.shape[1]), bf16)],
        scratch_shapes=[pltpu.VMEM((e, bq), f32), pltpu.VMEM((8, bq), f32), pltpu.VMEM((8, bq), f32), dma, dma((7, n_piece)), dma((7, n_piece))],
        compiler_params=params(1, collective_id=2),
        name="attn_fwd")(q, k, vt, g_own)


def bwd_kernel(q_ref, qt_ref, do_ref, dot_ref, o_ref, lse_ref, k_ref, v_ref, cos_ref, sin_ref, o_all, dwo_own,
               g_own, o_tok, g_tok, dwo_all, dlt, dqa, dka, dva, gqs, gks, gvs, loc_sem, o_send, o_recv, g_send, g_recv,
               w_sem, ag_send, ag_recv, *, bq, bk, t, nh, n_dev):
    h = pl.program_id(0)
    j = pl.program_id(1)
    nj = t // bk
    nq = t // bq
    rep = bk // D
    rows = t // n_dev
    early = nh - 1
    koff = pl.multiple_of(j * bk, bk)
    kc = pl.ds(koff, bk)
    me = lax.axis_index('sp')

    def rows_of(dev):
        return pl.ds(pl.multiple_of(dev * rows, rows), rows)

    def o_copy(rel):
        peer = peer_of(me, rel)
        return remote(o_all.at[rows_of(peer)], o_tok.at[me], (o_send, o_recv), rel, peer)

    def g_copy(head, rel):
        peer = peer_of(me, rel)
        return remote(gqs.at[head, rows_of(peer)], g_tok.at[me, :, pl.ds(head * D, D)],
                      (g_send.at[head], g_recv.at[head]), rel, peer)

    half = dwo_own.shape[0] // 2

    def own(n):
        return dwo_own.at[pl.ds(n * half, half)]

    def piece(owner, n):
        return dwo_all.at[pl.ds(pl.multiple_of((2 * owner + n) * half, half), half)]

    def w_copy(kind, n):
        return gather_copy(kind, n, own, piece, (ag_send, ag_recv), me)

    def w_local(n):
        return pltpu.make_async_copy(own(n), piece(me, n), w_sem.at[n])

    def o_local():
        return pltpu.make_async_copy(o_all.at[rows_of(me)], o_tok.at[me], loc_sem.at[0])

    def gq_local(head):
        return pltpu.make_async_copy(gqs.at[head], g_own.at[:, pl.ds(head * D, D)], loc_sem.at[1 + head])

    def gk_local(jj):
        r = pl.ds(jj * bk, bk)
        return pltpu.make_async_copy(gks.at[r], g_own.at[r, pl.ds(nh * D, D)], loc_sem.at[1 + nh + jj])

    def gv_local(jj):
        r = pl.ds(jj * bk, bk)
        return pltpu.make_async_copy(gvs.at[r], g_own.at[r, pl.ds((nh + 1) * D, D)], loc_sem.at[1 + nh + nj + jj])

    @pl.when((h == 0) & (j == 0))
    def _():
        meet_peers(me, n_dev)
        for rel in others(n_dev):
            o_copy(rel).start()
        o_local().start()
        for n in range(2):
            w_local(n).start()
            for kind in range(3):
                w_copy(kind, n).start()

    @pl.when((h == nh - 1) & (j == 0))
    def _():
        for n in range(2):
            w_copy(0, n).wait_recv()
            w_copy(1, n).wait_recv()
            for kind in (3, 4, 5):
                w_copy(kind, n).start()

    @pl.when(j == 0)
    def _():
        def init(i, carry):
            r = pl.ds(pl.multiple_of(i * bq, bq), bq)
            d = jnp.sum(do_ref[r, :].astype(f32) * o_ref[r, :].astype(f32), axis=1, keepdims=True)
            dlt[r, :] = jnp.broadcast_to(d, (bq, D))
            dqa[r, :] = jnp.zeros((bq, D), f32)
            return carry
        lax.fori_loop(0, nq, init, 0)

    @pl.when(h == 0)
    def _():
        dka[:, kc] = jnp.zeros((D, bk), f32)
        dva[:, kc] = jnp.zeros((D, bk), f32)

    def step(i, diag):
        off = pl.multiple_of(i * bq, bq)
        r = pl.ds(off, bq)
        nk = bk if diag is None else diag + bq
        rep = nk // D
        kc = pl.ds(koff, nk)
        kb, vb = k_ref[:nk, :], v_ref[:nk, :]
        s = lax.dot_general(q_ref[r, :], kb, NT, preferred_element_type=f32)
        dp = lax.dot_general(do_ref[r, :], vb, NT, preferred_element_type=f32)
        if diag is not None:
            qi = lax.broadcasted_iota(jnp.int32, (bq, nk), 0) + diag
            ki = lax.broadcasted_iota(jnp.int32, (bq, nk), 1)
            s = jnp.where(ki <= qi, s, -1e30)
        p = jnp.exp2(s * SCALE2 - jnp.concatenate([lse_ref[r, :]] * rep, axis=1))
        ds = ((dp - jnp.concatenate([dlt[r, :]] * rep, axis=1)) * p * SCALE).astype(bf16)
        dva[:, kc] += jnp.dot(dot_ref[:, r], p.astype(bf16), preferred_element_type=f32)
        dka[:, kc] += jnp.dot(qt_ref[:, r], ds, preferred_element_type=f32)
        dqa[r, :] += jnp.dot(ds, kb, preferred_element_type=f32)

    ratio = max(bk // bq, 1)
    first = (j * bk) // bq
    for d in range(ratio):
        step(first + d, d * bq)

    def body(i, carry):
        step(i, None)
        return carry

    lax.fori_loop(first + ratio, nq, body, 0)

    for head in range(nh):
        @pl.when((j == nj - 1) & (h == head))
        def _():
            def fin(i, carry):
                r = pl.ds(pl.multiple_of(i * bq, bq), bq)
                dq = dqa[r, :].astype(bf16).astype(f32)
                gqs[head, r, :] = rotate(dq, cos_ref[r, :], -sin_ref[r, :]).astype(bf16)
                return carry
            lax.fori_loop(0, nq, fin, 0)
            gq_local(head).start()
            if head < early:
                for rel in others(n_dev):
                    g_copy(head, rel).start()

    for jj in range(nj):
        @pl.when((h == nh - 1) & (j == jj))
        def _():
            dk = dka[:, jj * bk:(jj + 1) * bk].T.astype(bf16).astype(f32)
            r = slice(jj * bk, (jj + 1) * bk)
            gks[r, :] = rotate(dk, cos_ref[r, :], -sin_ref[r, :]).astype(bf16)
            gvs[r, :] = dva[:, jj * bk:(jj + 1) * bk].T.astype(bf16)
            gk_local(jj).start()
            gv_local(jj).start()

    @pl.when((h == nh - 1) & (j == nj - 1))
    def _():
        for n in range(2):
            w_local(n).wait()
            w_copy(3, n).wait_recv()
            w_copy(6, n).start()
        o_local().wait()
        for head in range(nh):
            gq_local(head).wait()
        for jj in range(nj):
            gk_local(jj).wait()
            gv_local(jj).wait()
        for rel in others(n_dev):
            o_copy(rel).wait()
            for head in range(early):
                g_copy(head, rel).wait()
        for n in range(2):
            for kind in (2, 4, 5, 6):
                w_copy(kind, n).wait_recv()
            for kind in range(7):
                w_copy(kind, n).wait_send()


def attn_bwd(q, qt, do, dot, o, lse, k, v, cos, sin, dwo, n_dev, bq=512, bk=1024):
    t, e = q.shape
    nh = e // D
    nj = t // bk
    rows = t // n_dev
    col = pl.BlockSpec((t, D), lambda h, j: (0, h))
    row_t = pl.BlockSpec((D, t), lambda h, j: (h, 0))
    kv_in = pl.BlockSpec((bk, D), lambda h, j: (j, 0))
    table = pl.BlockSpec((t, D), lambda h, j: (0, 0), pipeline_mode=pl.Buffered(1))
    return pl.pallas_call(
        functools.partial(bwd_kernel, bq=bq, bk=bk, t=t, nh=nh, n_dev=n_dev),
        grid=(nh, nj),
        in_specs=[col, row_t, col, row_t, col, col, kv_in, kv_in, table, table, hbm, hbm],
        out_specs=[hbm] * 4,
        out_shape=[shape((t, e + 2 * D), bf16), shape((n_dev, rows, e), bf16),
                   shape((n_dev, rows, (nh - 1) * D), bf16),
                   shape((n_dev * e, dwo.shape[1]), bf16)],
        scratch_shapes=[pltpu.VMEM((t, D), f32), pltpu.VMEM((t, D), f32), pltpu.VMEM((D, t), f32), pltpu.VMEM((D, t), f32),
                        pltpu.VMEM((nh, t, D), bf16), pltpu.VMEM((t, D), bf16), pltpu.VMEM((t, D), bf16),
                        dma((1 + nh + 2 * nj,)), dma((n_dev,)), dma((n_dev,)), dma((nh - 1, n_dev)), dma((nh - 1, n_dev)),
                        dma((2,)), dma((7, 2)), dma((7, 2))],
        compiler_params=params(2, collective_id=0),
        name="attn_bwd")(q, qt, do, dot, o, lse, k, v, cos, sin, o, dwo)


N_CHUNK = 6
K_STEP = 4
N_COL = 12
N_ROW = 6


def tail_kernel(h_ref, g_vm, wo_ref, wq_ref, wk_ref, wv_ref, x_ref, lnw_ref, g_own, g_tok, o_tok,
                a_ref, dx_ref, dl_ref, dw_all, g_late,
                gt, acc, stage, lhs, dh, dlw, a2a_send, a2a_recv, ag_send, ag_recv, dl_send, dl_recv, st_sem, lhs_sem,
                *, n_dev):
    step = pl.program_id(0)
    me = lax.axis_index('sp')
    t, width = g_vm.shape
    rows = t // n_dev
    qe = width - 2 * D
    early = g_tok.shape[2]
    late = width - early
    dim = x_ref.shape[1]
    chunk = dim // N_CHUNK
    kk = t // K_STEP
    s_a = N_CHUNK * K_STEP
    s_dh = s_a + N_COL
    s_ln = s_dh + N_COL
    cw = dim // N_COL
    last = s_ln + N_ROW - 1
    peers = [me] + [peer_of(me, rel) for rel in others(n_dev)]

    def rows_of(dev):
        return pl.ds(pl.multiple_of(dev * rows, rows), rows)

    def late_copy(rel):
        return remote(g_own.at[rows_of(peers[rel]), pl.ds(early, late)], g_late.at[me], (a2a_send, a2a_recv), rel, peers[rel])

    def piece(owner, n):
        return dw_all.at[pl.ds(pl.multiple_of(owner * dim + n * chunk, chunk), chunk)]

    def ag_copy(kind, n):
        return gather_copy(kind, n, lambda m: piece(me, m), piece, (ag_send, ag_recv), me)

    def dl_copy(rel):
        return remote(dlw.at[me], dlw.at[me], (dl_send, dl_recv), rel, peers[rel])

    def store_chunk(n):
        return pltpu.make_async_copy(stage.at[n % 2], piece(me, n), st_sem.at[n % 2])

    def o_load(rel):
        src = peers[rel]
        return pltpu.make_async_copy(o_tok.at[src], lhs.at[:, pl.ds(pl.multiple_of(src * qe, D), qe)], lhs_sem.at[0, rel])

    def g_load(rel):
        src = peers[rel]
        if rel == 0:
            first, second, base = g_own.at[rows_of(me), pl.ds(0, early)], g_own.at[rows_of(me)], early
        else:
            first, second, base = g_tok.at[src], g_late.at[src], 0
        n_q = qe - early
        col = pl.multiple_of(src * qe, D)
        kcol = pl.multiple_of(dim + src * D, D)
        vcol = pl.multiple_of(dim + n_dev * D + src * D, D)
        return [pltpu.make_async_copy(first, lhs.at[:, pl.ds(col, early)], lhs_sem.at[1, rel]),
                pltpu.make_async_copy(second.at[:, pl.ds(base, n_q)], lhs.at[:, pl.ds(col + early, n_q)], lhs_sem.at[2, rel]),
                pltpu.make_async_copy(second.at[:, pl.ds(base + n_q, D)], lhs.at[:, pl.ds(kcol, D)], lhs_sem.at[3, rel]),
                pltpu.make_async_copy(second.at[:, pl.ds(base + n_q + D, D)], lhs.at[:, pl.ds(vcol, D)], lhs_sem.at[4, rel])]

    @pl.when(step == 0)
    def _():
        meet_peers(me, n_dev)
        for rel in (6, 7, 2, 4, 3, 5, 1):
            late_copy(rel).start()
        for rel in range(n_dev):
            o_load(rel).start()

        def flip(i, carry):
            r = pl.ds(pl.multiple_of(i * 512, 512), 512)
            gt[:, r] = g_vm[r, :].T
            return carry
        lax.fori_loop(0, t // 512, flip, 0)

    for n in range(N_CHUNK):
        @pl.when(step == (n + 1) * K_STEP)
        def _():
            store_chunk(n).wait()
            for kind in range(3):
                ag_copy(kind, n).start()

    @pl.when(step < s_a)
    def _():
        k = step % K_STEP
        part = jnp.dot(gt[:, pl.ds(pl.multiple_of(k * kk, kk), kk)], h_ref[:], preferred_element_type=f32)

        @pl.when(k == 0)
        def _():
            acc[:] = part

        @pl.when(k > 0)
        def _():
            acc[:] += part

    for n in range(N_CHUNK):
        @pl.when(step == (n + 1) * K_STEP - 1)
        def _():
            stage[n % 2] = acc[:].T.astype(bf16)
            store_chunk(n).start()

    @pl.when(step == s_a)
    def _():
        for rel in range(n_dev):
            o_load(rel).wait()

    @pl.when((step >= s_a) & (step < s_dh))
    def _():
        a_ref[:] = jnp.dot(lhs[:, :dim], wo_ref[:], preferred_element_type=f32).astype(bf16)

    @pl.when(step == s_dh)
    def _():
        for rel in others(n_dev):
            late_copy(rel).wait_recv()
        for rel in range(n_dev):
            for copy in g_load(rel):
                copy.start()
        for rel in range(n_dev):
            for copy in g_load(rel):
                copy.wait()

    for n in range(N_COL):
        @pl.when(step == s_dh + n)
        def _():
            kv = n_dev * D
            dh[:, n * cw:(n + 1) * cw] = (
                lax.dot_general(lhs[:, :dim], wq_ref[:], NT, preferred_element_type=f32)
                + lax.dot_general(lhs[:, dim:dim + kv], wk_ref[:], NT, preferred_element_type=f32)
                + lax.dot_general(lhs[:, dim + kv:], wv_ref[:], NT, preferred_element_type=f32))

    @pl.when(step >= s_ln)
    def _():
        n = step - s_ln
        br = rows // N_ROW
        x = x_ref[:].astype(f32)
        grad = dh[pl.ds(pl.multiple_of(n * br, br), br), :]
        cen = x - jnp.mean(x, axis=1, keepdims=True)
        rstd = lax.rsqrt(jnp.mean(cen * cen, axis=1, keepdims=True) + LN_EPS)
        xhat = cen * rstd
        dy = grad * lnw_ref[:].astype(f32)
        m1 = jnp.mean(dy, axis=1, keepdims=True)
        m2 = jnp.mean(dy * xhat, axis=1, keepdims=True)
        dx_ref[:] = (rstd * (dy - m1 - xhat * m2)).astype(bf16)
        part = jnp.sum((grad * xhat).reshape(br // 8, 8, dim), axis=0)

        @pl.when(n == 0)
        def _():
            dlw[me] = part

        @pl.when(n > 0)
        def _():
            dlw[me] += part

    @pl.when(step == last)
    def _():
        for rel in others(n_dev):
            dl_copy(rel).start()
        for n in range(N_CHUNK):
            ag_copy(0, n).wait_recv()
            if n % 2 == 0:
                ag_copy(3, n).start()
            ag_copy(4, n).start()
            ag_copy(1, n).wait_recv()
            if n % 2 == 1:
                ag_copy(3, n).start()
            ag_copy(5, n).start()
        for n in range(N_CHUNK):
            ag_copy(3, n).wait_recv()
            ag_copy(6, n).start()
        for rel in others(n_dev):
            dl_copy(rel).wait()
            late_copy(rel).wait_send()
        total = dlw[0]
        for dev in others(n_dev):
            total = total + dlw[dev]
        dl_ref[:] = jnp.sum(total, axis=0, keepdims=True).astype(bf16)
        for n in range(N_CHUNK):
            for kind in (2, 4, 5, 6):
                ag_copy(kind, n).wait_recv()
        for n in range(N_CHUNK):
            for kind in range(7):
                ag_copy(kind, n).wait_send()


def tail(h_all, g_own, g_tok, o_tok, w_o, w_q, w_k, w_v, x, lnw, n_dev):
    t, dim = h_all.shape
    width = g_own.shape[1]
    rows = t // n_dev
    s_a = N_CHUNK * K_STEP
    s_dh = s_a + N_COL
    s_ln = s_dh + N_COL
    chunk, cw, br = dim // N_CHUNK, dim // N_COL, rows // N_ROW
    early = g_tok.shape[2]
    kv = w_k.shape[1]

    def h_map(s):
        c = jnp.minimum(s, s_a - 1)
        return c % K_STEP, c // K_STEP

    def at(first, count):
        return lambda s: jnp.clip(s - first, 0, count - 1)

    col_a, col_h, row_l = at(s_a, N_COL), at(s_dh, N_COL), at(s_ln, N_ROW)
    return pl.pallas_call(
        functools.partial(tail_kernel, n_dev=n_dev),
        grid=(s_ln + N_ROW,),
        in_specs=[pl.BlockSpec((t // K_STEP, chunk), h_map),
                  pl.BlockSpec((t, width), fixed, pipeline_mode=pl.Buffered(1)),
                  pl.BlockSpec((dim, cw), lambda s: (0, col_a(s))),
                  pl.BlockSpec((cw, dim), lambda s: (col_h(s), 0)),
                  pl.BlockSpec((cw, kv), lambda s: (col_h(s), 0)),
                  pl.BlockSpec((cw, kv), lambda s: (col_h(s), 0)),
                  pl.BlockSpec((br, dim), lambda s: (row_l(s), 0)),
                  pl.BlockSpec((1, dim), fixed),
                  hbm, hbm, hbm],
        out_specs=[pl.BlockSpec((rows, cw), lambda s: (0, col_a(s))),
                   pl.BlockSpec((br, dim), lambda s: (row_l(s), 0)),
                   pl.BlockSpec((1, dim), fixed),
                   hbm, hbm],
        out_shape=[shape((rows, dim), bf16), shape((rows, dim), bf16),
                   shape((1, dim), bf16), shape((n_dev * dim, width), bf16),
                   shape((n_dev, rows, width - early), bf16)],
        scratch_shapes=[pltpu.VMEM((width, t), bf16), pltpu.VMEM((width, chunk), f32), pltpu.VMEM((2, chunk, width), bf16),
                        pltpu.VMEM((rows, dim + 2 * kv), bf16), pltpu.VMEM((rows, dim), f32), pltpu.VMEM((n_dev, 8, dim), f32),
                        dma((n_dev,)), dma((n_dev,)), dma((7, N_CHUNK)), dma((7, N_CHUNK)),
                        dma((n_dev,)), dma((n_dev,)), dma((2,)), dma((5, n_dev))],
        compiler_params=params(1, collective_id=1),
        name="tail")(h_all, g_own, w_o, w_q, w_k, w_v, x, lnw, g_own, g_tok, o_tok)


def spread_kernel(src_ref, a_ref, dx_ref, wo_ref, q_ref, k_ref, v_ref, a_out, dx_out, wo_out):
    n_dev, _, width = src_ref.shape
    qe = width - 2 * D
    for dev in range(n_dev):
        q_ref[:, dev * qe:(dev + 1) * qe] = src_ref[dev, :, :qe]
        k_ref[:, dev * D:(dev + 1) * D] = src_ref[dev, :, qe:qe + D]
        v_ref[:, dev * D:(dev + 1) * D] = src_ref[dev, :, qe + D:]
    a_out[:] = a_ref[:]
    dx_out[:] = dx_ref[:]
    wo_out[:] = wo_ref[:]


def spread(dw_all, a, dx, dwo, steps=12):
    n_dev, dim, width = dw_all.shape
    bt = dim // steps
    qe = width - 2 * D
    same = [(x, pl.BlockSpec((x.shape[0] // steps, x.shape[1]), rows_at)) for x in (a, dx, dwo)]
    cols = [n_dev * c for c in (qe, D, D)]
    return pl.pallas_call(
        spread_kernel,
        grid=(steps,),
        in_specs=[pl.BlockSpec((n_dev, bt, width), lambda i: (0, i, 0))] + [spec for _, spec in same],
        out_specs=[pl.BlockSpec((bt, c), rows_at) for c in cols] + [spec for _, spec in same],
        out_shape=[shape((dim, c), bf16) for c in cols] + [shape(x.shape, bf16) for x, _ in same],
        compiler_params=params(),
        name="spread")(dw_all, a, dx, dwo)


def solution(mesh):
    n_dev = mesh.shape['sp']
    row_spec = P(('dp', 'sp'), None)
    pos_spec = P(('dp', 'sp'))
    full_spec = P(None, None)
    grad_spec = P('dp', None)

    def local_step(hidden, positions, d_attn, ln_weight, w_q, w_k, w_v, w_o):
        rows, dim = hidden.shape
        qe = w_q.shape[1] // n_dev
        ke = w_k.shape[1] // n_dev
        lane = jnp.arange(D, dtype=jnp.int32)
        freq = ROPE_BASE ** (-(lane - lane % 2).astype(f32) / D)
        pos = jnp.pad(positions.reshape(N_SUB, rows // N_SUB // D, D), ((0, 0), (0, 8 - rows // N_SUB // D), (0, 0)))
        q, qt, k, v, vt, cos, sin, h_all = start(hidden, ln_weight.reshape(1, dim), w_q, w_k, w_v, freq.reshape(1, D), pos, qe // D, n_dev)
        o, ot, lse, g_first = attn_fwd(q, k, vt, d_attn, rows * 2 // 3, n_dev)
        do, dot, dwo_own, _ = mid(g_first, ot, w_o, d_attn, n_dev)
        g_own, o_tok, g_tok, dw_o = attn_bwd(q, qt, do, dot, o, lse, k, v, cos, sin, dwo_own, n_dev)
        attn_out, d_hid, d_lnw, dw_all, _ = tail(h_all, g_own, g_tok, o_tok, w_o, w_q, w_k, w_v, hidden,
                                                 ln_weight.reshape(1, dim), n_dev)
        dw_q, dw_k, dw_v, attn_out, d_hid, dw_o = spread(dw_all.reshape(n_dev, dim, qe + 2 * ke), attn_out, d_hid, dw_o)
        return attn_out, d_hid, d_lnw.reshape(dim), dw_q, dw_k, dw_v, dw_o

    return jax.shard_map(local_step, mesh=mesh,
                         in_specs=(row_spec, pos_spec, row_spec, P(None), full_spec, full_spec, full_spec, full_spec),
                         out_specs=(row_spec, row_spec, P('dp'), grad_spec, grad_spec, grad_spec, grad_spec),
                         check_vma=False)
```

time: 876 us -> 787 us (0.90)
  Pallas kernels: 590 us -> 775 us
  waiting for transfers between devices: 177 us -> 0 us
  local copies, waits for them, and re-layouts: 27.3 us -> 2.6 us
  other arithmetic: 25.7 us -> 1.16 us
  matrix products: 22.2 us -> 0 us
  blocking collectives: 14 us -> 0 us
  between operations: 14.2 us -> 0.87 us
    pallas_call x4, Pallas kernels: 195 us -> 393 us  [the longest x1 171 us: start(): pl.pallas_call(functools.partial(start_kernel, n_dev=n_dev, nh=nh), grid=...]
    all_gather x3 -> x0, waiting for transfers between devices: 177 us -> none  [the longest x1 143 us: local_step(): h_all = lax.all_gather(normed, 'sp', axis=0, tiled=True)]
    dot_general x1 -> x0, matrix products: 22.2 us -> none  [local_step(): jnp.einsum('te,td->ed', o, g_all, preferred_element_type=f32).astype(bf16)]
    unnamed x14 -> x2, local copies, waits for them, and re-layouts: 20 us -> 0.01 us
    all_gather x1 -> x0, blocking collectives: 14 us -> none  [local_step(): cos, sin = rope_tables(lax.all_gather(positions, 'sp', axis=0, tiled=True))]
    select_n x1 -> x0, other arithmetic: 13.7 us -> none  [rope_tables(): return (jnp.cos(angles), jnp.where(lane[None, :] % 2 == 0, -sin, sin))]
    pallas_call x1, Pallas kernels: 197 us -> 183 us  [attn_bwd(): pl.pallas_call(functools.partial(bwd_kernel, bq=bq, bk=bk, t=t, nh=nh, n_...]
  transfers between devices with their start and end apart: 3 -> 0, of which waited for: 2 -> 0; matrix products, arithmetic and copies ran while one was open for 3% -> 0% of each run, Pallas kernels for 68% -> 0%
where the time goes in v3:
time: 787 us; the launch traced here: 780 us
  Pallas kernels  775 us (98%)
    pallas_call x1, Pallas kernels, tail(): pl.pallas_call(functools.partial(tail_kernel, n_dev=n_dev), grid=(s_ln +...  199 us
    pallas_call x1, Pallas kernels, attn_bwd(): pl.pallas_call(functools.partial(bwd_kernel, bq=bq, bk=bk, t=t, nh=nh, n_...  183 us
    pallas_call x1, Pallas kernels, start(): pl.pallas_call(functools.partial(start_kernel, n_dev=n_dev, nh=nh), grid=...  171 us
    pallas_call x1, Pallas kernels, attn_fwd(): pl.pallas_call(functools.partial(fwd_kernel, bq=bq, bk=bk, nh=nh, n_dev=n...  112 us
    pallas_call x1, Pallas kernels, mid(): pl.pallas_call(functools.partial(mid_kernel, n_dev=n_dev, rows=rows, firs...  69.8 us
    pallas_call x1, Pallas kernels, spread(): pl.pallas_call(spread_kernel, grid=(steps,), in_specs=[pl.BlockSpec((n_de...  39.9 us

profile of v3, /device:TPU:0, one launch (start us, length us, event | category | flops | bytes accessed | tf_op | source)
XLA Modules:
  0.0 779.6 jit_solution(4752388592577788667)
XLA Ops:
  0.6 0.5 fusion.3.freq_ref
  1.2 0.7 reshape.69
  1.9 0.6 pad.4.pos_ref
  2.5 1.3 reshape.68.lnw_ref
  3.8 170.7 %start.1 = (bf16[6144,384]{1,0:T(8,128)(2,1)}, bf16[384,6144]{1,0:T(8,128)(2,1)}, bf16[6144,128]{1,0:T(8,128)(2,1)}, bf16[6144,128]{1,0:T(8,128)(2,1)}, bf16[128...) custom-call(bf16[768,3072]{1,0:T(8,128)(2,1)} %x_ref.3, ...), custom_call_target="tpu_custom_call" | custom-call | tf_op jit(solution)/shard_map/start/pallas_call | solution.py:242
  174.5 112.4 %attn_fwd.1 = (bf16[6144,384]{1,0:T(8,128)(2,1)}, bf16[384,6144]{1,0:T(8,128)(2,1)}, f32[6144,384]{1,0:T(8,128)}, bf16[4096,3072]{1,0:T(8,128)(2,1)}) custom-call(bf16[6144,384]{1,0:T(8,128)(2,1)} %get-tuple-element.37.q_ref, bf16[6144,128]{1,0:T(8,128)(2,1)} %get-tuple-element.39.k_ref, bf16[128,6144]{1,0:T(8,128)(2,1)} %get-tuple-element.40.vt_ref, ...), custom_call_target="tpu_custom_call" | custom-call | tf_op jit(solution)/shard_map/attn_fwd/pallas_call | solution.py:461
  286.9 69.8 %mid.1 = (bf16[6144,384]{1,0:T(8,128)(2,1)}, bf16[384,6144]{1,0:T(8,128)(2,1)}, bf16[384,3072]{1,0:T(8,128)(2,1)}, bf16[2048,3072]{1,0:T(8,128)(2,1)}) custom-call(bf16[4096,3072]{1,0:T(8,128)(2,1)} %get-tuple-element.41.g_blk, bf16[384,6144]{1,0:T(8,128)(2,1)} %get-tuple-element.42.ot_ref, bf16[3072,3072]{1,0:T(8,128)(2,1)} %wo_ref.1, bf16[768,3072]{1,0:T(8,128)(2,1)} %g_own.3), custom_call_target="tpu_custom_call" | custom-call | tf_op jit(solution)/shard_map/mid/pallas_call | solution.py:344
  356.7 183.4 %attn_bwd.1 = (bf16[6144,640]{1,0:T(8,128)(2,1)}, bf16[8,768,384]{2,1,0:T(8,128)(2,1)}, bf16[8,768,256]{2,1,0:T(8,128)(2,1)}, bf16[3072,3072]{1,0:T(8,128)(2,1)}) custom-call(bf16[6144,384]{1,0:T(8,128)(2,1)} %get-tuple-element.37.q_ref, bf16[384,6144]{1,0:T(8,128)(2,1)} %get-tuple-element.38.qt_ref, bf16[6144,384]{1,0:T(8,128)(2,1)} %get-tuple-element.43.do_ref, ...), custom_call_target="tpu_custom_call" | custom-call | tf_op jit(solution)/shard_map/attn_bwd/pallas_call | solution.py:647
  540.0 198.8 %tail.1 = (bf16[768,3072]{1,0:T(8,128)(2,1)}, bf16[768,3072]{1,0:T(8,128)(2,1)}, bf16[1,3072]{1,0:T(2,128)(2,1)}, bf16[24576,640]{1,0:T(8,128)(2,1)}, bf16[8,768,384]{2,1,0:T(8,128)(2,1)}) custom-call(bf16[6144,3072]{1,0:T(8,128)(2,1)} %get-tuple-element.36.h_ref, bf16[6144,640]{1,0:T(8,128)(2,1)} %get-tuple-element.51.g_vm.g_own, ...), custom_call_target="tpu_custom_call" | custom-call | tf_op jit(solution)/shard_map/tail/pallas_call | solution.py:869
  738.9 0.0 copy-start
  738.9 39.9 %spread.1 = (bf16[3072,3072]{1,0:T(8,128)(2,1)}, bf16[3072,1024]{1,0:T(8,128)(2,1)}, bf16[3072,1024]{1,0:T(8,128)(2,1)}, bf16[768,3072]{1,0:T(8,128)(2,1)}, bf16...) custom-call(bf16[8,3072,640]{2,1,0:T(8,128)(2,1)} %bitcast.1, bf16[768,3072]{1,0:T(8,128)(2,1)} %get-tuple-element.55.a_ref, ...), custom_call_target="tpu_custom_call" | custom-call | tf_op jit(solution)/shard_map/spread/pallas_call | solution.py:914
  778.8 0.0 copy-done
  778.8 0.6 reduce
Async XLA Ops:
  738.9 39.9 %copy-start = (bf16[1,3072]{1,0:T(2,128)(2,1)S(1)}, bf16[1,3072]{1,0:T(2,128)(2,1)}, u32[]{:S(2)}) copy-start(bf16[1,3072]{1,0:T(2,128)(2,1)} %get-tuple-element.60) | copy-start | bytes 18436

commit v4 on v3

--- a/solution.py
+++ b/solution.py
@@ -252,7 +252,7 @@
         name="start")(x, lnw, w_q, w_k, w_v, freq, pos)
 
 
-def mid_kernel(g_blk, ot_ref, w_ref, g_own, do_ref, dot_ref, dwo_ref, g_rest, acc, buf, ld_sem, ag_send, ag_recv, *, n_dev, rows, first):
+def mid_kernel(g_blk, ot_hbm, w_hbm, g_own, do_ref, dot_ref, dwo_ref, g_rest, ot_ref, w_ref, op_sem, acc, buf, ld_sem, ag_send, ag_recv, *, n_dev, rows, first):
     step = pl.program_id(0)
     me = lax.axis_index('sp')
     rest = rows - first
@@ -286,7 +286,14 @@
         for n in range(2):
             for kind in range(3):
                 copy(kind, n).start()
+        e = w_ref.shape[0]
+        fetch = [pltpu.make_async_copy(ot_hbm, ot_ref, op_sem.at[0]),
+                 pltpu.make_async_copy(w_hbm.at[pl.ds(pl.multiple_of(me * e, D), e)], w_ref, op_sem.at[1])]
+        for copy_in in fetch:
+            copy_in.start()
         acc[:] = jnp.zeros_like(acc)
+        for copy_in in fetch:
+            copy_in.wait()
 
     @pl.when(step == 5)
     def _():
@@ -318,11 +325,14 @@
     def _():
         compute(g_blk[:], pl.multiple_of(step * rows, D), first)
 
-    for i in range(n_dev):
-        @pl.when(step == n_dev + i)
-        def _():
-            load(i).wait()
-            compute(buf[i % 2], pl.multiple_of(peer_of(me, order[i]) * rows + first, D), rest)
+    @pl.when(step >= n_dev)
+    def _():
+        i = step - n_dev
+        u = i - XN
+        rel = jnp.where((u >= 0) & (u < 4), XN + 2 * (u % 2) + u // 2, i)
+        slot = i % 2
+        pltpu.make_async_copy(g_own.at[pl.ds(first, rest)], buf.at[slot], ld_sem.at[slot]).wait()
+        compute(buf[slot], pl.multiple_of(peer_of(me, rel) * rows + first, D), rest)
 
     @pl.when(step == 2 * n_dev - 1)
     def _():
@@ -338,17 +348,16 @@
     first = g_first.shape[0] // n_dev
     rest = rows - first
     e, t = ot.shape
-    whole = lambda a, b: pl.BlockSpec((a, b), fixed, pipeline_mode=pl.Buffered(1))
     const = lambda a, b: pl.BlockSpec((a, b), fixed)
-    w_spec = pl.BlockSpec((e, dim), lambda i: (lax.axis_index('sp'), 0), pipeline_mode=pl.Buffered(1))
     return pl.pallas_call(
         functools.partial(mid_kernel, n_dev=n_dev, rows=rows, first=first),
         grid=(2 * n_dev,),
-        in_specs=[pl.BlockSpec((first, dim), lambda i: (jnp.minimum(i, n_dev - 1), 0)), whole(e, t), w_spec, hbm],
+        in_specs=[pl.BlockSpec((first, dim), lambda i: (jnp.minimum(i, n_dev - 1), 0)), hbm, hbm, hbm],
         out_specs=[const(t, e), const(e, t), const(e, dim), hbm],
         out_shape=[shape((t, e), bf16), shape((e, t), bf16), shape((e, dim), bf16),
                    shape((n_dev * rest, dim), bf16)],
-        scratch_shapes=[pltpu.VMEM((e, dim), f32), pltpu.VMEM((2, rest, dim), bf16), dma((2,)), dma((7, 2)), dma((7, 2))],
+        scratch_shapes=[pltpu.VMEM((e, t), bf16), pltpu.VMEM((e, dim), bf16), dma((2,)),
+                        pltpu.VMEM((e, dim), f32), pltpu.VMEM((2, rest, dim), bf16), dma((2,)), dma((7, 2)), dma((7, 2))],
         compiler_params=params(1, collective_id=3),
         name="mid")(g_first, ot, w, g_own)
 
@@ -666,9 +675,9 @@
 N_ROW = 6
 
 
-def tail_kernel(h_ref, g_vm, wo_ref, wq_ref, wk_ref, wv_ref, x_ref, lnw_ref, g_own, g_tok, o_tok,
+def tail_kernel(h_ref, wo_ref, wq_ref, wk_ref, wv_ref, x_ref, lnw_ref, g_own, g_tok, o_tok,
                 a_ref, dx_ref, dl_ref, dw_all, g_late,
-                gt, acc, stage, lhs, dh, dlw, a2a_send, a2a_recv, ag_send, ag_recv, dl_send, dl_recv, st_sem, lhs_sem,
+                g_vm, g_sem, gt, acc, stage, lhs, dh, dlw, a2a_send, a2a_recv, ag_send, ag_recv, dl_send, dl_recv, st_sem, lhs_sem,
                 *, n_dev):
     step = pl.program_id(0)
     me = lax.axis_index('sp')
@@ -731,6 +740,9 @@
             late_copy(rel).start()
         for rel in range(n_dev):
             o_load(rel).start()
+        fetch = pltpu.make_async_copy(g_own, g_vm, g_sem)
+        fetch.start()
+        fetch.wait()
 
         def flip(i, carry):
             r = pl.ds(pl.multiple_of(i * 512, 512), 512)
@@ -758,11 +770,11 @@
         def _():
             acc[:] += part
 
-    for n in range(N_CHUNK):
-        @pl.when(step == (n + 1) * K_STEP - 1)
-        def _():
-            stage[n % 2] = acc[:].T.astype(bf16)
-            store_chunk(n).start()
+    @pl.when((step < s_a) & (step % K_STEP == K_STEP - 1))
+    def _():
+        n = step // K_STEP
+        stage[n % 2] = acc[:].T.astype(bf16)
+        store_chunk(n).start()
 
     @pl.when(step == s_a)
     def _():
@@ -784,14 +796,13 @@
             for copy in g_load(rel):
                 copy.wait()
 
-    for n in range(N_COL):
-        @pl.when(step == s_dh + n)
-        def _():
-            kv = n_dev * D
-            dh[:, n * cw:(n + 1) * cw] = (
-                lax.dot_general(lhs[:, :dim], wq_ref[:], NT, preferred_element_type=f32)
-                + lax.dot_general(lhs[:, dim:dim + kv], wk_ref[:], NT, preferred_element_type=f32)
-                + lax.dot_general(lhs[:, dim + kv:], wv_ref[:], NT, preferred_element_type=f32))
+    @pl.when((step >= s_dh) & (step < s_ln))
+    def _():
+        kv = n_dev * D
+        dh[:, pl.ds(pl.multiple_of((step - s_dh) * cw, cw), cw)] = (
+            lax.dot_general(lhs[:, :dim], wq_ref[:], NT, preferred_element_type=f32)
+            + lax.dot_general(lhs[:, dim:dim + kv], wk_ref[:], NT, preferred_element_type=f32)
+            + lax.dot_general(lhs[:, dim + kv:], wv_ref[:], NT, preferred_element_type=f32))
 
     @pl.when(step >= s_ln)
     def _():
@@ -870,7 +881,6 @@
         functools.partial(tail_kernel, n_dev=n_dev),
         grid=(s_ln + N_ROW,),
         in_specs=[pl.BlockSpec((t // K_STEP, chunk), h_map),
-                  pl.BlockSpec((t, width), fixed, pipeline_mode=pl.Buffered(1)),
                   pl.BlockSpec((dim, cw), lambda s: (0, col_a(s))),
                   pl.BlockSpec((cw, dim), lambda s: (col_h(s), 0)),
                   pl.BlockSpec((cw, kv), lambda s: (col_h(s), 0)),
@@ -885,12 +895,12 @@
         out_shape=[shape((rows, dim), bf16), shape((rows, dim), bf16),
                    shape((1, dim), bf16), shape((n_dev * dim, width), bf16),
                    shape((n_dev, rows, width - early), bf16)],
-        scratch_shapes=[pltpu.VMEM((width, t), bf16), pltpu.VMEM((width, chunk), f32), pltpu.VMEM((2, chunk, width), bf16),
+        scratch_shapes=[pltpu.VMEM((t, width), bf16), dma, pltpu.VMEM((width, t), bf16), pltpu.VMEM((width, chunk), f32), pltpu.VMEM((2, chunk, width), bf16),
                         pltpu.VMEM((rows, dim + 2 * kv), bf16), pltpu.VMEM((rows, dim), f32), pltpu.VMEM((n_dev, 8, dim), f32),
                         dma((n_dev,)), dma((n_dev,)), dma((7, N_CHUNK)), dma((7, N_CHUNK)),
                         dma((n_dev,)), dma((n_dev,)), dma((2,)), dma((5, n_dev))],
         compiler_params=params(1, collective_id=1),
-        name="tail")(h_all, g_own, w_o, w_q, w_k, w_v, x, lnw, g_own, g_tok, o_tok)
+        name="tail")(h_all, w_o, w_q, w_k, w_v, x, lnw, g_own, g_tok, o_tok)
 
 
 def spread_kernel(src_ref, a_ref, dx_ref, wo_ref, q_ref, k_ref, v_ref, a_out, dx_out, wo_out):

time: 787 us -> 775 us (0.985)
  no operation moved by 1% of the time
where the time goes in v4:
time: 775 us
  Pallas kernels  770 us (99%)
    pallas_call x1, Pallas kernels, tail(): pl.pallas_call(functools.partial(tail_kernel, n_dev=n_dev), grid=(s_ln +...  196 us
    pallas_call x1, Pallas kernels, attn_bwd(): pl.pallas_call(functools.partial(bwd_kernel, bq=bq, bk=bk, t=t, nh=nh, n_...  183 us
    pallas_call x1, Pallas kernels, start(): pl.pallas_call(functools.partial(start_kernel, n_dev=n_dev, nh=nh), grid=...  171 us
    pallas_call x1, Pallas kernels, attn_fwd(): pl.pallas_call(functools.partial(fwd_kernel, bq=bq, bk=bk, nh=nh, n_dev=n...  112 us
    pallas_call x1, Pallas kernels, mid(): pl.pallas_call(functools.partial(mid_kernel, n_dev=n_dev, rows=rows, firs...  67.5 us
    pallas_call x1, Pallas kernels, spread(): pl.pallas_call(spread_kernel, grid=(steps,), in_specs=[pl.BlockSpec((n_de...  39.9 us

profile of v4, /device:TPU:0, one launch (start us, length us, event | category | flops | bytes accessed | tf_op | source)
XLA Modules:
  0.0 774.8 jit_solution(10006675303770874167)
XLA Ops:
  0.6 0.5 fusion.3.freq_ref
  1.2 0.7 reshape.69
  1.9 0.6 pad.4.pos_ref
  2.5 1.3 reshape.68.lnw_ref
  3.8 170.7 %start.1 = (bf16[6144,384]{1,0:T(8,128)(2,1)}, bf16[384,6144]{1,0:T(8,128)(2,1)}, bf16[6144,128]{1,0:T(8,128)(2,1)}, bf16[6144,128]{1,0:T(8,128)(2,1)}, bf16[128...) custom-call(bf16[768,3072]{1,0:T(8,128)(2,1)} %x_ref.3, ...), custom_call_target="tpu_custom_call" | custom-call | tf_op jit(solution)/shard_map/start/pallas_call | solution.py:242
  174.5 112.4 %attn_fwd.1 = (bf16[6144,384]{1,0:T(8,128)(2,1)}, bf16[384,6144]{1,0:T(8,128)(2,1)}, f32[6144,384]{1,0:T(8,128)}, bf16[4096,3072]{1,0:T(8,128)(2,1)}) custom-call(bf16[6144,384]{1,0:T(8,128)(2,1)} %get-tuple-element.37.q_ref, bf16[6144,128]{1,0:T(8,128)(2,1)} %get-tuple-element.39.k_ref, bf16[128,6144]{1,0:T(8,128)(2,1)} %get-tuple-element.40.vt_ref, ...), custom_call_target="tpu_custom_call" | custom-call | tf_op jit(solution)/shard_map/attn_fwd/pallas_call | solution.py:470
  286.9 67.5 %mid.1 = (bf16[6144,384]{1,0:T(8,128)(2,1)}, bf16[384,6144]{1,0:T(8,128)(2,1)}, bf16[384,3072]{1,0:T(8,128)(2,1)}, bf16[2048,3072]{1,0:T(8,128)(2,1)}) custom-call(bf16[4096,3072]{1,0:T(8,128)(2,1)} %get-tuple-element.41.g_blk, bf16[384,6144]{1,0:T(8,128)(2,1)} %get-tuple-element.42.ot_hbm, bf16[3072,3072]{1,0:T(8,128)(2,1)} %wo_ref.1, bf16[768,3072]{1,0:T(8,128)(2,1)} %g_own.3), custom_call_target="tpu_custom_call" | custom-call | tf_op jit(solution)/shard_map/mid/pallas_call | solution.py:352
  354.4 183.4 %attn_bwd.1 = (bf16[6144,640]{1,0:T(8,128)(2,1)}, bf16[8,768,384]{2,1,0:T(8,128)(2,1)}, bf16[8,768,256]{2,1,0:T(8,128)(2,1)}, bf16[3072,3072]{1,0:T(8,128)(2,1)}) custom-call(bf16[6144,384]{1,0:T(8,128)(2,1)} %get-tuple-element.37.q_ref, bf16[384,6144]{1,0:T(8,128)(2,1)} %get-tuple-element.38.qt_ref, bf16[6144,384]{1,0:T(8,128)(2,1)} %get-tuple-element.43.do_ref, ...), custom_call_target="tpu_custom_call" | custom-call | tf_op jit(solution)/shard_map/attn_bwd/pallas_call | solution.py:656
  537.8 196.5 %tail.1 = (bf16[768,3072]{1,0:T(8,128)(2,1)}, bf16[768,3072]{1,0:T(8,128)(2,1)}, bf16[1,3072]{1,0:T(2,128)(2,1)}, bf16[24576,640]{1,0:T(8,128)(2,1)}, bf16[8,768,384]{2,1,0:T(8,128)(2,1)}) custom-call(bf16[6144,3072]{1,0:T(8,128)(2,1)} %get-tuple-element.36.h_ref, bf16[3072,3072]{1,0:T(8,128)(2,1)} %wo_ref.1, bf16[3072,3072]{1,0:T(8,128)(2,1)} %wq_ref.1, ...), custom_call_target="tpu_custom_call" | custom-call | tf_op jit(solution)/shard_map/tail/pallas_call | solution.py:880
  734.3 0.0 copy-start
  734.3 39.9 %spread.1 = (bf16[3072,3072]{1,0:T(8,128)(2,1)}, bf16[3072,1024]{1,0:T(8,128)(2,1)}, bf16[3072,1024]{1,0:T(8,128)(2,1)}, bf16[768,3072]{1,0:T(8,128)(2,1)}, bf16...) custom-call(bf16[8,3072,640]{2,1,0:T(8,128)(2,1)} %bitcast.1, bf16[768,3072]{1,0:T(8,128)(2,1)} %get-tuple-element.55.a_ref, ...), custom_call_target="tpu_custom_call" | custom-call | tf_op jit(solution)/shard_map/spread/pallas_call | solution.py:924
  774.2 0.0 copy-done
  774.2 0.6 reduce
Async XLA Ops:
  734.3 39.9 %copy-start = (bf16[1,3072]{1,0:T(2,128)(2,1)S(1)}, bf16[1,3072]{1,0:T(2,128)(2,1)}, u32[]{:S(2)}) copy-start(bf16[1,3072]{1,0:T(2,128)(2,1)} %get-tuple-element.60) | copy-start | bytes 18436
